TPU v7x, 256 devices: a whole 4x4x8 slice. The times are simulated.
256 devices in a mesh: pop: 8 (over x_lo, y), dp: 32 (over z, x_hi, core).
Axes of the slice: x: 4 (x_hi: 2, x_lo: 2; x = x_hi * 2 + x_lo), y: 4, z: 8, core: 2. Of those that a mesh axis runs over, the one named last changes fastest.
Arguments:
- observations: bfloat16 [8, 16384, 256], P('pop', 'dp'), may hold values from -6 to 6
- returns: float32 [8, 16384], P('pop', 'dp'), may hold values from 0 to 2
- actions: int32 [8, 16384], P('pop', 'dp'), may hold values from 0 to 17
- w_input: bfloat16 [8, 256, 2048], P('pop', 'dp'), may hold values from -0.375 to 0.375
- w_middle: bfloat16 [8, 2048, 2048], P('pop', 'dp'), may hold values from -0.125 to 0.125
- w_head: bfloat16 [8, 2048, 18], P('pop', 'dp'), may hold values from -0.125 to 0.125
- log_rate: float32 [8], replicated, may hold values from 3 to 4
- copy_from: int32 [8], replicated, may hold values from 0 to 1, as said below
- perturb: int32 [8], replicated, may hold values from 0 to 2
Outputs:
- next_input: bfloat16 [8, 256, 2048], P('pop', 'dp')
- next_middle: bfloat16 [8, 2048, 2048], P('pop', 'dp')
- next_head: bfloat16 [8, 2048, 18], P('pop', 'dp')
- next_log_rate: float32 [8], P('pop')
- fitness: float32 [8], P('pop')
Inputs may be any that keep to these rules, and one draw needn't show every extreme that they name: Some two members that lie 4 apart have copy_from 1.
All inputs are finite; a program needn't handle non-finite values.
Results may differ from a plain program's by a relative error of at most 0.014.
Values may be sent and summed in bfloat16 or wider, within the bound.
A program may use at most 128 MiB of HBM per device.

v0:
```python
import jax
import jax.numpy as jnp
from jax import lax
from jax.sharding import PartitionSpec as P

CAP = 2.0


def joined_along(parts, dim):
    parts = jnp.moveaxis(parts, 0, dim)
    lengths = parts.shape
    return parts.reshape(*lengths[:dim], lengths[dim] * lengths[dim + 1], *lengths[dim + 2 :])


def gather_packed(arrays, axis, dims):
    line = jnp.concatenate([a.reshape(-1) for a in arrays])
    lines, at, done = (lax.all_gather(line, axis), 0, [])
    for a, dim in zip(arrays, dims):
        parts = lines[:, at : at + a.size].reshape(-1, *a.shape)
        done.append(joined_along(parts, dim))
        at += a.size
    return tuple(done)


def from_everyone(shard, axis):
    peers = lax.axis_size(axis)
    return lax.all_to_all(
        jnp.broadcast_to(shard[None], (peers, *shard.shape)), axis, 0, 0, tiled=True
    )


def of_everyone(shard, axis):
    everything = from_everyone(shard, axis)
    return jnp.sum(everything, axis=0)


def in_blocks(shard, dim, peers):
    before, after = (shard.shape[:dim], shard.shape[dim + 1 :])
    return jnp.moveaxis(shard.reshape(*before, peers, -1, *after), dim, 0)


def sum_at_owner(shard, axis, dim):
    peers = lax.axis_size(axis)
    parts = lax.all_to_all(in_blocks(shard, dim, peers), axis, 0, 0, tiled=True)
    return jnp.sum(parts.astype(jnp.float32), axis=0)


def shifted(block, axis, distance):
    devices = range(lax.axis_size(axis))
    route = [((i - distance) % len(devices), i) for i in devices]
    return lax.ppermute(block, axis, route)


def silu_slope(pre):
    sig = jax.nn.sigmoid(pre)
    return sig * (1.0 + pre * (1.0 - sig))


def contract_rows(left, right):
    return lax.dot_general(
        left, right, (((0,), (0,)), ((), ())), preferred_element_type=jnp.float32
    )


def contract_cols(left, right):
    return lax.dot_general(
        left, right, (((1,), (1,)), ((), ())), preferred_element_type=jnp.float32
    )


def local(observations, returns, actions, w_input, w_middle, w_head, log_rate, copy_from, perturb):
    obs = observations[0]
    gains = returns[0]
    chosen = actions[0]
    own_first = w_input[0]
    own_middle = w_middle[0]
    own_head = w_head[0]
    rows = obs.shape[0]
    batch = rows * lax.axis_size("dp")
    first, head = gather_packed((own_first, own_head), "dp", (0, 0))
    pre1 = jnp.dot(obs, first, preferred_element_type=jnp.float32)
    hidden1 = jax.nn.silu(pre1).astype(jnp.bfloat16)
    whole = lax.all_gather(own_middle, "dp", axis=0, tiled=True)
    pre2 = jnp.dot(hidden1, whole, preferred_element_type=jnp.float32)
    hidden2 = jax.nn.silu(pre2).astype(jnp.bfloat16)
    squash = jnp.tanh(jnp.dot(hidden2, head, preferred_element_type=jnp.float32) / CAP)
    logits = CAP * squash
    logp = logits - jnp.log(jnp.sum(jnp.exp(logits), axis=1, keepdims=True))
    onehot = (chosen[:, None] == lax.broadcasted_iota(jnp.int32, logits.shape, 1)).astype(
        jnp.float32
    )
    taken = jnp.sum(logp * onehot, axis=1)
    fitness = of_everyone(jnp.sum(gains * taken) / batch, "dp")
    grad_raw = (
        -(gains / batch)[:, None] * (onehot - jnp.exp(logp)) * (1.0 - squash * squash)
    ).astype(jnp.bfloat16)
    head_term = contract_rows(hidden2, grad_raw)
    grad_pre2 = (contract_cols(grad_raw, head) * silu_slope(pre2)).astype(jnp.bfloat16)
    grad_middle = lax.psum_scatter(
        contract_rows(hidden1, grad_pre2).astype(jnp.bfloat16),
        "dp",
        scatter_dimension=0,
        tiled=True,
    ).astype(jnp.float32)
    member = lax.axis_index("pop")
    members = lax.axis_size("pop")
    rate = jnp.exp(lax.dynamic_index_in_dim(log_rate, member, keepdims=False))
    new_middle = (own_middle.astype(jnp.float32) - rate * grad_middle).astype(jnp.bfloat16)
    back = contract_cols(grad_pre2, whole)
    grad_pre1 = (back * silu_slope(pre1)).astype(jnp.bfloat16)
    input_term = contract_rows(obs, grad_pre1)
    grad_first, grad_head = (
        sum_at_owner(input_term.astype(jnp.bfloat16), "dp", 0),
        sum_at_owner(head_term.astype(jnp.bfloat16), "dp", 0),
    )
    new_first = (own_first.astype(jnp.float32) - rate * grad_first).astype(jnp.bfloat16)
    new_head = (own_head.astype(jnp.float32) - rate * grad_head).astype(jnp.bfloat16)
    moved_first, moved_middle, moved_head = shifted((new_first, new_middle, new_head), "pop", 1)
    flag = lax.dynamic_index_in_dim(copy_from, member, keepdims=False) == 1
    out_first = jnp.where(flag, moved_first, new_first)
    out_middle = jnp.where(flag, moved_middle, new_middle)
    out_head = jnp.where(flag, moved_head, new_head)
    source = jnp.where(flag, (member + members - 1) % members, member)
    pick = lax.dynamic_index_in_dim(perturb, member, keepdims=False)
    offset = jnp.where(pick == 0, -0.2, jnp.where(pick == 1, 0.0, 0.2)).astype(jnp.float32)
    next_rate = lax.dynamic_index_in_dim(log_rate, source, keepdims=False) + offset
    return (
        out_first[None],
        out_middle[None],
        out_head[None],
        next_rate.reshape(1),
        fitness.reshape(1),
    )


def solution(mesh):
    in_specs = (
        P("pop", "dp", None),
        P("pop", "dp"),
        P("pop", "dp"),
        P("pop", "dp", None),
        P("pop", "dp", None),
        P("pop", "dp", None),
        P(),
        P(),
        P(),
    )
    out_specs = (
        P("pop", "dp", None),
        P("pop", "dp", None),
        P("pop", "dp", None),
        P("pop"),
        P("pop"),
    )
    return jax.shard_map(local, mesh=mesh, in_specs=in_specs, out_specs=out_specs, check_vma=False)
```

profile of v0, /device:TPU:1, one launch (start us, length us, event | category | flops | bytes accessed | tf_op | source)
XLA Modules:
  0.0 385.9 jit_solution(15649825401868657893)
XLA Ops:
  7.2 0.8 copy.37
  8.2 0.8 copy.50
  10.5 85.2 %all-gather.8.cloned.1.call-done = bf16[32,1,17536]{2,1,0:T(2,128)(2,1)} async-done(((bf16[1,1,17536]{2,1,0:T(2,128)(2,1)}), bf16[32,1,17536]{2,1,0:T(2,128)(2,1)}) %all-gather.8.cloned.1.call-update) | async-done | bytes 1122320 | tf_op jit(solution)/shard_map/all_gather | solution.py:17
  95.6 1.8 copy.53
  98.0 1.2 reshape_reshape.7
  99.3 2.7 fusion.20
  102.0 94.5 %all-gather.6.cloned.1.call-done = bf16[1,2048,2048]{2,1,0:T(8,128)(2,1)} async-done(((bf16[1,64,2048]{2,1,0:T(8,128)(2,1)}), bf16[1,2048,2048]{2,1,0:T(8,128)(2,1)}) %all-gather.6.cloned.1.call-update) | async-done | bytes 8388624 | tf_op jit(solution)/shard_map/all_gather | solution.py:83
  196.4 9.0 %multiply_convert_fusion.1 = (bf16[512,2048]{0,1:T(8,128)(2,1)S(1)}, f32[512,2048]{0,1:T(8,128)S(1)}) fusion(bf16[1,2048,2048]{2,1,0:T(8,128)(2,1)} %all-gather.6.cloned.1.call-done, f32[2048,512]{1,0:T(8,128)} %fusion.20), kind=kOutput, calls=%fused_computation.17 | convolution fusion | flops 4305453056 | bytes 18874368 | tf_op jit(solution)/shard_map/dot_general | solution.py:84
  206.6 1.7 multiply_convert_fusion
  208.2 1.3 copy-done.10
  209.6 6.9 %convolution_convert_fusion = bf16[2048,2048]{1,0:T(8,128)(2,1)} fusion(bf16[512,2048]{0,1:T(8,128)(2,1)S(1)} %multiply_convert_fusion, f32[2048,512]{1,0:T(8,128)S(1)} %copy-done.1), kind=kOutput, calls=%fused_computation.4 | convolution fusion | flops 4304404480 | bytes 14680064 | tf_op jit(solution)/shard_map/dot_general | solution.py:60
  217.8 4.6 %all-to-all-start.2 = ((f32[32,1,1]{2,1,0:T(1,128)}), f32[32,1,1]{2,1,0:T(1,128)S(1)}, u32[]{:S(2)}, u32[]{:S(2)}) async-start(f32[32,1,1]{2,1,0:T(1,128)} %broadcast_in_dim.20), calls=%async_computation.3 | async-start | bytes 32768 | tf_op jit(solution)/shard_map/all_to_all | solution.py:27
  223.4 0.8 reshape.64
  224.1 7.6 %all-to-all-done.2 = f32[32,1,1]{2,1,0:T(1,128)S(1)} async-done(((f32[32,1,1]{2,1,0:T(1,128)}), f32[32,1,1]{2,1,0:T(1,128)S(1)}, u32[]{:S(2)}, u32[]{:S(2)}) %all-to-all-start.2) | async-done | bytes 160 | tf_op jit(solution)/shard_map/all_to_all | solution.py:27
  231.7 4.1 %all-to-all-start.1 = ((bf16[32,2,576]{2,1,0:T(2,128)(2,1)}), bf16[32,2,576]{2,1,0:T(2,128)(2,1)S(1)}, u32[]{:S(2)}, u32[]{:S(2)}) async-start(bf16[32,2,576]{2,1,0:T(2,128)(2,1)} %reshape.64), calls=%async_computation.2 | async-start | bytes 163840 | tf_op jit(solution)/shard_map/all_to_all | solution.py:44
  235.9 12.9 %fusion.14 = bf16[32,8,2048]{2,1,0:T(8,128)(2,1)} fusion(f32[2048,512]{1,0:T(8,128)} %fusion.20, bf16[512,2048]{0,1:T(8,128)(2,1)} %copy-done.10, bf16[1,2048,2048]{2,1,0:T(8,128)(2,1)} %all-gather.6.cloned.1.call-done, bf16[1,512,256]{2,1,0:T(8,128)(2,1)S(1)} %copy-done), kind=kOutput, calls=%fused_computation.20 | convolution fusion | flops 4841799680 | bytes 15990784 | tf_op jit(solution)/shard_map/dot_general | solution.py:60
  248.9 9.9 %all-to-all-start = ((bf16[32,8,2048]{2,1,0:T(8,128)(2,1)}), bf16[32,8,2048]{2,1,0:T(8,128)(2,1)S(1)}, u32[]{:S(2)}, u32[]{:S(2)}) async-start(bf16[32,8,2048]{2,1,0:T(8,128)(2,1)} %fusion.14), calls=%async_computation | async-start | bytes 2097152 | tf_op jit(solution)/shard_map/all_to_all | solution.py:44
  261.6 1.3 collective-permute-start.2
  267.2 24.3 %all-to-all-done = bf16[32,8,2048]{2,1,0:T(8,128)(2,1)S(1)} async-done(((bf16[32,8,2048]{2,1,0:T(8,128)(2,1)}), bf16[32,8,2048]{2,1,0:T(8,128)(2,1)S(1)}, u32[]{:S(2)}, u32[]{:S(2)}) %all-to-all-start) | async-done | bytes 1048608 | tf_op jit(solution)/shard_map/all_to_all | solution.py:44
  291.6 1.3 collective-permute-start
  292.9 76.2 %reduce-scatter.2.cloned.1.call-done = bf16[64,2048]{1,0:T(8,128)(2,1)} async-done(((bf16[2048,2048]{1,0:T(8,128)(2,1)}), bf16[64,2048]{1,0:T(8,128)(2,1)}) %reduce-scatter.2.cloned.1.call-update) | async-done | bytes 262160 | tf_op jit(solution)/shard_map/reduce_scatter | solution.py:99
  369.1 1.0 fusion.18
  370.1 1.3 collective-permute-start.1
  372.1 5.4 %collective-permute-done.1 = bf16[64,2048]{1,0:T(8,128)(2,1)S(1)} collective-permute-done((bf16[64,2048]{1,0:T(8,128)(2,1)S(1)}, bf16[64,2048]{1,0:T(8,128)(2,1)S(1)}, u32[]{:S(2)}, u32[]{:S(2)}) %collective-permute-start.1) | collective-permute-done | bytes 262176 | tf_op jit(solution)/shard_map/ppermute | solution.py:51
  (56 shorter events, 10.3 us)
Async XLA Ops:
  7.2 92.1 %copy-start = (bf16[1,512,256]{2,1,0:T(8,128)(2,1)S(1)}, bf16[1,512,256]{2,1,0:T(8,128)(2,1)}, u32[]{:S(2)}) copy-start(bf16[1,512,256]{2,1,0:T(8,128)(2,1)} %param.9) | copy-start | bytes 786436
  7.2 88.5 %all-gather.8.cloned.1.call-start = ((), (), s32[]{:S(2)}) async-start(), calls=%async_computation.6 | async-start | bytes 2314752 | tf_op jit(solution)/shard_map/all_gather | solution.py:17
  9.7 186.8 %all-gather.6.cloned.1.call-start = ((), (), s32[]{:S(2)}) async-start(), calls=%async_computation.5 | async-start | bytes 8650752 | tf_op jit(solution)/shard_map/all_gather | solution.py:83
  10.4 358.6 %reduce-scatter.2.cloned.1.call-start = ((), (), s32[]{:S(2)}) async-start(), calls=%async_computation.4 | async-start | bytes 8650752 | tf_op jit(solution)/shard_map/reduce_scatter | solution.py:99
  102.0 103.9 %copy-start.5 = (s32[1,512]{1,0:T(1,128)S(1)}, s32[1,512]{1,0:T(1,128)}, u32[]{:S(2)}) copy-start(s32[1,512]{1,0:T(1,128)} %param.11) | copy-start | bytes 6148
  102.0 104.0 %copy-start.7 = (f32[1,512]{1,0:T(1,128)S(1)}, f32[1,512]{1,0:T(1,128)}, u32[]{:S(2)}) copy-start(f32[1,512]{1,0:T(1,128)} %param.10) | copy-start | bytes 6148
  206.6 3.0 copy-start.1
  208.2 1.3 copy-start.10
  217.8 14.0 %all-to-all-start.2 = ((f32[32,1,1]{2,1,0:T(1,128)}), f32[32,1,1]{2,1,0:T(1,128)S(1)}, u32[]{:S(2)}, u32[]{:S(2)}) async-start(f32[32,1,1]{2,1,0:T(1,128)} %broadcast_in_dim.20), calls=%async_computation.3 | async-start | bytes 32768 | tf_op jit(solution)/shard_map/all_to_all | solution.py:27
  231.7 17.1 %all-to-all-start.1 = ((bf16[32,2,576]{2,1,0:T(2,128)(2,1)}), bf16[32,2,576]{2,1,0:T(2,128)(2,1)S(1)}, u32[]{:S(2)}, u32[]{:S(2)}) async-start(bf16[32,2,576]{2,1,0:T(2,128)(2,1)} %reshape.64), calls=%async_computation.2 | async-start | bytes 163840 | tf_op jit(solution)/shard_map/all_to_all | solution.py:44
  235.9 22.9 %copy-start.8 = (s32[8]{0:T(128)S(1)}, s32[8]{0:T(128)}, u32[]{:S(2)}) copy-start(s32[8]{0:T(128)} %param.16) | copy-start | bytes 100
  235.9 24.1 %copy-start.6 = (f32[8]{0:T(128)S(1)}, f32[8]{0:T(128)}, u32[]{:S(2)}) copy-start(f32[8]{0:T(128)} %param.15) | copy-start | bytes 100
  235.9 25.6 %copy-start.4 = (bf16[1,64,18]{1,2,0:T(8,128)(2,1)S(1)}, bf16[1,64,18]{1,2,0:T(8,128)(2,1)}, u32[]{:S(2)}) copy-start(bf16[1,64,18]{1,2,0:T(8,128)(2,1)} %param.14) | copy-start | bytes 6916
  235.9 26.9 %copy-start.9 = (s32[8]{0:T(128)S(1)}, s32[8]{0:T(128)}, u32[]{:S(2)}) copy-start(s32[8]{0:T(128)} %param.17) | copy-start | bytes 100
  235.9 55.7 %copy-start.3 = (bf16[1,8,2048]{2,1,0:T(8,128)(2,1)S(1)}, bf16[1,8,2048]{2,1,0:T(8,128)(2,1)}, u32[]{:S(2)}) copy-start(bf16[1,8,2048]{2,1,0:T(8,128)(2,1)} %param.12) | copy-start | bytes 98308
  235.9 133.1 %copy-start.2 = (bf16[1,64,2048]{2,1,0:T(8,128)(2,1)S(1)}, bf16[1,64,2048]{2,1,0:T(8,128)(2,1)}, u32[]{:S(2)}) copy-start(bf16[1,64,2048]{2,1,0:T(8,128)(2,1)} %param.13) | copy-start | bytes 786436
  248.9 42.6 %all-to-all-start = ((bf16[32,8,2048]{2,1,0:T(8,128)(2,1)}), bf16[32,8,2048]{2,1,0:T(8,128)(2,1)S(1)}, u32[]{:S(2)}, u32[]{:S(2)}) async-start(bf16[32,8,2048]{2,1,0:T(8,128)(2,1)} %fusion.14), calls=%async_computation | async-start | bytes 2097152 | tf_op jit(solution)/shard_map/all_to_all | solution.py:44
  261.6 5.0 %collective-permute-start.2 = (bf16[64,18]{0,1:T(8,128)(2,1)S(1)}, bf16[64,18]{0,1:T(8,128)(2,1)S(1)}, u32[]{:S(2)}, u32[]{:S(2)}) collective-permute-start(bf16[64,18]{0,1:T(8,128)(2,1)S(1)} %fusion.23), channel_id=1, source_target_pairs={{224,0},{0,32},{32,64},{64,96},{96,128},{128,160},{160,192},{192,2... | collective-permute-start | bytes 6920 | tf_op jit(solution)/shard_map/ppermute | solution.py:51
  291.6 79.8 %collective-permute-start = (bf16[8,2048]{1,0:T(8,128)(2,1)S(1)}, bf16[8,2048]{1,0:T(8,128)(2,1)S(1)}, u32[]{:S(2)}, u32[]{:S(2)}) collective-permute-start(bf16[8,2048]{1,0:T(8,128)(2,1)S(1)} %fusion.22), channel_id=1, source_target_pairs={{224,0},{0,32},{32,64},{64,96},{96,128},{128,160},{160,192},{192,2... | collective-permute-start | bytes 98312 | tf_op jit(solution)/shard_map/ppermute | solution.py:51
  370.1 7.4 %collective-permute-start.1 = (bf16[64,2048]{1,0:T(8,128)(2,1)S(1)}, bf16[64,2048]{1,0:T(8,128)(2,1)S(1)}, u32[]{:S(2)}, u32[]{:S(2)}) collective-permute-start(bf16[64,2048]{1,0:T(8,128)(2,1)S(1)} %fusion.18), channel_id=1, source_target_pairs={{224,0},{0,32},{32,64},{64,96},{96,128},{128,160},{160,192},{192,2... | collective-permute-start | bytes 786440 | tf_op jit(solution)/shard_map/ppermute | solution.py:51
Sparse Core Ops, SparseCore 0:
  11.3 84.3 all-gather.7
  98.4 97.9 all-gather.5
  216.6 152.3 reduce-scatter.1
where the time goes:
time: 390 us; the launch traced here: 386 us
  waiting for transfers between devices  294 us (75%)
  matrix products  34.3 us (9%)
  starting transfers between devices  22.7 us (6%)
  between operations  19.1 us (5%)
  local copies, waits for them, and re-layouts  11 us (3%)
  other arithmetic  4.48 us (1%)
    all_gather x1, waiting for transfers between devices, local(): whole = lax.all_gather(own_middle, 'dp', axis=0, tiled=True)  94.5 us
    all_gather x1, waiting for transfers between devices, gather_packed(): lines, at, done = (lax.all_gather(line, axis), 0, [])  85.2 us
    reduce_scatter x1, waiting for transfers between devices, local(): lax.psum_scatter(contract_rows(hidden1, grad_pre2).astype(jnp.bfloat16),...  76.2 us
    all_to_all x2, waiting for transfers between devices, sum_at_owner(): parts = lax.all_to_all(in_blocks(shard, dim, peers), axis, 0, 0, tiled=True)  24.3 us
    dot_general x3, matrix products, contract_rows(): lax.dot_general(left, right, (((0,), (0,)), ((), ())), preferred_element_...  20.5 us
    all_to_all x2, starting transfers between devices, sum_at_owner(): parts = lax.all_to_all(in_blocks(shard, dim, peers), axis, 0, 0, tiled=True)  14 us
    dot_general x1, matrix products, local(): pre2 = jnp.dot(hidden1, whole, preferred_element_type=jnp.float32)  8.98 us
  transfers between devices with their start and end apart: 9, of which 7 were waited for; matrix products, arithmetic and copies ran while one was open for 7% of the time, Pallas kernels for 0%

commit v1 on v0

v1 whole, which is shorter than its diff:
```python
import jax
import jax.numpy as jnp
from jax import lax
from jax.experimental import pallas as pl
from jax.experimental.pallas import tpu as pltpu
from jax.sharding import PartitionSpec as P

F32 = jnp.float32
BF16 = jnp.bfloat16
Z = 8
K = Z // 2
Q = 4
ROWS = 512
OBS = 256
D = 2048
QC = D // Q
BK = D // Z
ACT = 18
POP = 8
BATCH = ROWS * Z * Q
WI, WM, WH = 0, 1, 2
OB, QT, RAW, GR, DH, OUT = range(6)
RIGHT, LEFT = 0, 1


def nt(a, b):
    return lax.dot_general(a, b, (((1,), (1,)), ((), ())), preferred_element_type=F32)


def nn(a, b):
    return jnp.dot(a, b, preferred_element_type=F32)


def kernel(
    obs, ret, act, win, wmid, whead, lrate, copyf, pert,
    o_in, o_mid, o_head, o_rate, o_fit,
    ob, obT, wi, wh, wq, w1T, wT, h1, s1, p2, h2, g2, whq, whT,
    raw_s, raw_r, gr, dW, rss, rsb, dI, sib_s, sib_r, ris, rib, tin, xs, xr,
    dH, dHg, tH, nm, ym, om, ni, yi, nh, yh,
    ag_s, ag_r, gp_s, gp_r, xp_s, xp_r, sb_s, sb_r, dh_s, dh_r, rs_s, rs_r, ri_s, ri_r, y_s, y_r, loc,
):
    m = lax.axis_index("pop")
    d = lax.axis_index("dp")
    z = d // Q
    q = lax.rem(d, Q)
    h = q // 2
    c = lax.rem(q, 2)
    sib = {"dp": z * Q + h * 2 + (1 - c)}
    xpt = {"dp": z * Q + (1 - h) * 2 + c}
    side = [{"dp": lax.rem(z + 1, Z) * Q + q}, {"dp": lax.rem(z + Z - 1, Z) * Q + q}]
    after = {"pop": lax.rem(m + 1, POP)}
    before = {"pop": lax.rem(m + POP - 1, POP)}

    def mate(t):
        return lax.rem(q + t, Q)

    def mate_id(t):
        return {"dp": z * Q + mate(t)}

    def at(off):
        return lax.rem(z + off + Z, Z)

    def copy(src, dst, ss, rs, dev):
        return pltpu.make_async_remote_copy(
            src_ref=src, dst_ref=dst, send_sem=ss, recv_sem=rs, device_id=dev,
            device_id_type=pl.DeviceIdType.MESH,
        )

    fetch = [
        pltpu.make_async_copy(win, wi.at[z, h, c], loc.at[0]),
        pltpu.make_async_copy(wmid.at[:, pl.ds(pl.multiple_of(q * QC, QC), QC)], wq.at[z, q], loc.at[1]),
        pltpu.make_async_copy(whead, wh.at[z, h, c], loc.at[2]),
        pltpu.make_async_copy(obs, ob.at[q], loc.at[3]),
    ]
    for f in fetch:
        f.start()

    barrier = pltpu.get_barrier_semaphore()
    for dev in [mate_id(1), mate_id(2), mate_id(3), side[0], side[1], after, before]:
        pl.semaphore_signal(barrier, inc=1, device_id=dev, device_id_type=pl.DeviceIdType.MESH)
    pl.semaphore_wait(barrier, 7)

    xwi = copy(win, wi.at[z, h, c], xp_s.at[0], xp_r.at[0], xpt)
    xwi.start()
    xwh = copy(whead, wh.at[z, h, c], xp_s.at[1], xp_r.at[1], xpt)

    def quarter(t):
        p = mate(t)
        return copy(
            wmid.at[:, pl.ds(pl.multiple_of(p * QC, QC), QC)], wq.at[z, q], gp_s.at[QT, p], gp_r.at[QT, q], mate_id(t)
        )

    def sight(t):
        return copy(obs, ob.at[q], gp_s.at[OB, mate(t)], gp_r.at[OB, q], mate_id(t))

    def quarter_in(p):
        copy(wq.at[z, p], wq.at[z, p], gp_s.at[QT, p], gp_r.at[QT, p], sib).wait_recv()

    for t in (1, 2, 3):
        quarter(t).start()
    xwh.start()
    for t in (1, 2, 3):
        sight(t).start()

    def piece(kind, b, j):
        if kind == WI:
            return wi.at[b, j, c]
        if kind == WM:
            return wq.at[b, pl.ds(2 * j, 2)]
        return wh.at[b, j, c]

    def ag(kind, way, k, j):
        b = at(1 - k) if way == RIGHT else at(k - 1)
        ref = piece(kind, b, j)
        return copy(ref, ref, ag_s.at[kind, way, k - 1, j], ag_r.at[kind, way, k - 1, j], side[way])

    def ag_in(kind, way, k, j):
        b = at(-k) if way == RIGHT else at(k)
        ref = piece(kind, b, j)
        copy(ref, ref, ag_s.at[kind, way, k - 1, j], ag_r.at[kind, way, k - 1, j], side[way]).wait_recv()

    def put(kinds, k, j):
        for kind in kinds:
            for way in (RIGHT, LEFT):
                ag(kind, way, k, j).start()

    def take(kinds, k, j):
        for kind in kinds:
            for way in (RIGHT, LEFT):
                ag_in(kind, way, k, j)

    def take_last(kinds, k):
        for kind in kinds:
            ag_in(kind, RIGHT, k, 0)
            ag_in(kind, LEFT, k, 1)

    def put_last(kinds):
        for kind in kinds:
            ag(kind, RIGHT, K, 0).start()
            ag(kind, LEFT, K, 1).start()

    MID = (WM, WH)
    fetch[0].wait()
    put((WI,), 1, h)
    fetch[1].wait()
    fetch[2].wait()
    quarter_in(h * 2 + (1 - c))
    put(MID, 1, h)
    xwi.wait_recv()
    put((WI,), 1, 1 - h)
    take((WI,), 1, h)
    put((WI,), 2, h)
    quarter_in((1 - h) * 2)
    quarter_in((1 - h) * 2 + 1)
    xwh.wait_recv()
    put(MID, 1, 1 - h)
    take((WI,), 1, 1 - h)
    put((WI,), 2, 1 - h)

    fetch[3].wait()
    for t in (1, 2, 3):
        p = mate(t)
        copy(ob.at[p], ob.at[p], gp_s.at[OB, p], gp_r.at[OB, p], sib).wait_recv()

    def turn(i, _):
        x = ob[i].astype(F32)
        obT[:, pl.ds(pl.multiple_of(i * ROWS, ROWS), ROWS)] = jnp.transpose(x).astype(BF16)
        return 0

    lax.fori_loop(0, Q, turn, 0)
    take((WI,), 2, h)
    put((WI,), 3, h)
    take(MID, 1, h)
    put(MID, 2, h)
    take((WI,), 2, 1 - h)
    put((WI,), 3, 1 - h)
    take_last((WI,), 3)
    put_last((WI,))
    ag_in(WI, RIGHT, 3, 1)
    ag_in(WI, LEFT, 3, 0)
    take(MID, 1, 1 - h)
    put(MID, 2, 1 - h)
    take_last((WI,), K)

    def core_copy(ref, i):
        return copy(ref.at[:, :, c], ref.at[:, :, c], sb_s.at[i], sb_r.at[i], sib)

    def core_in(ref, i):
        copy(ref.at[:, :, 1 - c], ref.at[:, :, 1 - c], sb_s.at[i], sb_r.at[i], sib).wait_recv()

    core_copy(wi, 0).start()
    core_in(wi, 0)

    def turn_in(i, _):
        cols = pl.ds(pl.multiple_of(i * 256, 256), 256)
        x = wi[:, :, :, :, cols].astype(F32).reshape(OBS, 256)
        w1T[cols, :] = jnp.transpose(x).astype(BF16)
        return 0

    lax.fori_loop(0, D // 256, turn_in, 0)

    def unit(i, _):
        @pl.when(i == 1)
        def _():
            take(MID, 2, h)
            put(MID, 3, h)

        @pl.when(i == 2)
        def _():
            take(MID, 2, 1 - h)
            put(MID, 3, 1 - h)

        @pl.when(i == 4)
        def _():
            take_last(MID, 3)
            put_last(MID)

        @pl.when(i == 5)
        def _():
            for kind in MID:
                ag_in(kind, RIGHT, 3, 1)
                ag_in(kind, LEFT, 3, 0)

        @pl.when(i == 7)
        def _():
            take_last(MID, K)
            core_copy(wh, 1).start()

        b = at(((i + 1) // 2) * (2 * lax.rem(i + 1, 2) - 1))
        feats = pl.ds(pl.multiple_of(b * BK, BK), BK)
        wT[...] = jnp.transpose(wq[b].astype(F32).reshape(BK, QC)).astype(BF16)

        def tile(r, _):
            rows = pl.ds(pl.multiple_of(r * 256, 256), 256)
            v = nn(w1T[feats, :], obT[:, rows])
            s = 0.5 * jnp.tanh(0.5 * v) + 0.5
            hid = v * s
            hb = hid.astype(BF16)
            h1[feats, rows] = hb
            s1[feats, rows] = (s + hid * (1.0 - s)).astype(BF16)
            add = nn(wT[...], hb)
            p2[:, rows] = jnp.where(jnp.full(add.shape, i) == 0, add, p2[:, rows] + add)
            return 0

        lax.fori_loop(0, D // 256, tile, 0)
        return 0

    p2[...] = jnp.zeros_like(p2)
    lax.fori_loop(0, Z, unit, 0)

    core_in(wh, 1)
    whq[...] = jnp.zeros_like(whq)
    for i in range(2):
        whq[i * 256 : (i + 1) * 256, 0:ACT] = wh[2 * q + i].astype(F32).reshape(256, ACT)
    whT[...] = jnp.transpose(whq[...])[0:32, :].astype(BF16)

    def raw_out(p):
        return copy(raw_s.at[p], raw_r.at[q], gp_s.at[RAW, p], gp_r.at[RAW, q], {"dp": z * Q + p})

    for t in (2, 1, 3, 0):
        p = mate(t)
        rows = pl.ds(pl.multiple_of(p * ROWS, ROWS), ROWS)

        def forward2(i, _):
            cols = pl.ds(pl.multiple_of(p * ROWS + i * 128, 128), 128)
            v = p2[:, cols]
            s = 0.5 * jnp.tanh(0.5 * v) + 0.5
            hid = v * s
            h2[:, cols] = hid.astype(BF16)
            p2[:, cols] = s + hid * (1.0 - s)
            return 0

        lax.fori_loop(0, 4, forward2, 0)
        raw_s[p] = nn(whT[...], h2[:, rows])[0:24, :]
        if t:
            raw_out(p).start()
    raw = raw_s[q]
    for t in (2, 1, 3):
        p = mate(t)
        copy(raw_r.at[p], raw_r.at[p], gp_s.at[RAW, p], gp_r.at[RAW, p], sib).wait_recv()
        raw = raw + raw_r[p]
    at_act = lax.broadcasted_iota(jnp.int32, raw.shape, 0)
    squash = jnp.tanh(raw * 0.5)
    logits = 2.0 * squash
    e = jnp.where(at_act < ACT, jnp.exp(logits), 0.0)
    total = jnp.sum(e, axis=0, keepdims=True)
    logp = logits - jnp.log(total)
    onehot = jnp.where(at_act == act[...], 1.0, 0.0)
    gains = ret[...] * (1.0 / BATCH)
    term = gains * jnp.sum(logp * onehot, axis=0, keepdims=True)
    grad = -gains * (onehot - e / total) * (1.0 - squash * squash)
    high = term.astype(BF16).astype(F32)
    low = term - high
    grad = jnp.where(at_act < ACT, grad, jnp.where(at_act == ACT, high, jnp.where(at_act == ACT + 1, low, 0.0)))
    gr[q] = jnp.concatenate([grad, jnp.zeros((8, ROWS), F32)], axis=0).astype(BF16)

    def gr_out(t):
        return copy(gr.at[q], gr.at[q], gp_s.at[GR, mate(t)], gp_r.at[GR, q], mate_id(t))

    for t in (2, 1, 3):
        gr_out(t).start()
    wb = whq[...].astype(BF16)[:, 0:32]
    for t in (0, 1, 2, 3):
        p = mate(t)
        if t:
            copy(gr.at[p], gr.at[p], gp_s.at[GR, p], gp_r.at[GR, p], sib).wait_recv()
        rows = pl.ds(pl.multiple_of(p * ROWS, ROWS), ROWS)
        g2[:, rows] = (nn(wb, gr[p]) * p2[:, rows]).astype(BF16)

    def middle(i, _):
        b = at(K + ((i + 1) // 2) * (1 - 2 * lax.rem(i, 2)))
        feats = pl.ds(pl.multiple_of(b * BK, BK), BK)
        dW[b] = nt(h1[feats, :], g2[...]).reshape(Q, BK // Q, QC)
        return 0

    def rs_copy(way, k, p):
        return copy(
            rss.at[way, k - 1, p], rsb.at[way, k - 1, p], rs_s.at[way, k - 1, p], rs_r.at[way, k - 1, p], side[way]
        )

    def rs_in(way, k, p):
        copy(rsb.at[way, k, p], rsb.at[way, k, p], rs_s.at[way, k, p], rs_r.at[way, k, p], side[way]).wait_recv()
        return rsb[way, k, p].astype(F32)

    def rs_put(way, k, p, joined):
        v = dW[at(k if way == RIGHT else -k), p]
        if joined:
            v = v + rs_in(way, k, p)
        rss[way, k - 1, p] = v.astype(BF16)
        rs_copy(way, k, p).start()

    lax.fori_loop(0, 3, middle, 0)

    def rs_open(j, _):
        rs_put(RIGHT, K, j, False)
        rs_put(LEFT, K, 2 + j, False)
        return 0

    def rs_open2(j, _):
        rs_put(RIGHT, K - 1, 2 + j, False)
        rs_put(LEFT, K - 1, j, False)
        return 0

    lax.fori_loop(0, 2, rs_open, 0)
    lax.fori_loop(0, 2, rs_open2, 0)
    lax.fori_loop(3, Z, middle, 0)

    acc = jnp.zeros((32, QC), F32)
    fit = jnp.zeros((1, ROWS), F32)
    for p in range(Q):
        acc = acc + nt(gr[p], h2[:, p * ROWS : (p + 1) * ROWS])
        x = gr[p].astype(F32)
        fit = fit + x[ACT : ACT + 1, :] + x[ACT + 1 : ACT + 2, :]
    at_head = lax.broadcasted_iota(jnp.int32, (24, QC), 0)
    dH[z] = jnp.where(at_head == ACT, fit, acc[0:24, :])

    def dh_copy(way, k):
        b = at(1 - k) if way == RIGHT else at(k - 1)
        return copy(dH.at[b], dH.at[b], dh_s.at[way, k - 1], dh_r.at[way, k - 1], side[way])

    def dh_in(way, k):
        b = at(-k) if way == RIGHT else at(k)
        copy(dH.at[b], dH.at[b], dh_s.at[way, k - 1], dh_r.at[way, k - 1], side[way]).wait_recv()

    dh_copy(RIGHT, 1).start()
    dh_copy(LEFT, 1).start()

    def rs_join(j, _):
        rs_put(RIGHT, K - 1, j, True)
        rs_put(LEFT, K - 1, 2 + j, True)
        return 0

    lax.fori_loop(0, 2, rs_join, 0)

    def back(i, _):
        k = 2 - i // 4
        p = lax.rem(i, 4)

        feats = pl.ds(pl.multiple_of(i * 256, 256), 256)
        w = wq[i].reshape(BK, QC)

        def tile(r, acc):
            rows = pl.ds(pl.multiple_of(r * ROWS, ROWS), ROWS)
            g = (nn(w, g2[:, rows]) * s1[feats, rows].astype(F32)).astype(BF16)
            return acc + nt(obT[:, rows], g)

        dI[:, :, :, :, feats] = lax.fori_loop(0, Q, tile, jnp.zeros((OBS, 256), F32)).reshape(Z, 2, 2, 8, 256)
        rs_put(RIGHT, k, p, True)
        rs_put(LEFT, k, p, True)

        @pl.when(i == 2)
        def _():
            dh_in(RIGHT, 1)
            dh_in(LEFT, 1)
            dh_copy(RIGHT, 2).start()
            dh_copy(LEFT, 2).start()

        @pl.when(i == 4)
        def _():
            dh_in(RIGHT, 2)
            dh_in(LEFT, 2)
            dh_copy(RIGHT, 3).start()
            dh_copy(LEFT, 3).start()

        @pl.when(i == 6)
        def _():
            dh_in(RIGHT, 3)
            dh_in(LEFT, 3)
            dh_copy(RIGHT, 4).start()

        return 0

    lax.fori_loop(0, Z, back, 0)

    for b in range(Z):
        for j in range(2):
            sib_s[b, j] = dI[b, j, 1 - c].astype(BF16)
    core_sum = copy(sib_s, sib_r, sb_s.at[2], sb_r.at[2], sib)
    core_sum.start()
    core_sum.wait_recv()

    def own_in(off, j):
        b = at(off)
        return dI[b, j, c] + sib_r[b, j].astype(F32)

    def ri_copy(way, k, j):
        return copy(
            ris.at[way, k - 1, j], rib.at[way, k - 1, j], ri_s.at[way, k - 1, j], ri_r.at[way, k - 1, j], side[way]
        )

    def ri_in(way, k, j):
        copy(rib.at[way, k, j], rib.at[way, k, j], ri_s.at[way, k, j], ri_r.at[way, k, j], side[way]).wait_recv()
        return rib[way, k, j].astype(F32)

    def ri_put(way, k, j, joined):
        v = own_in(k if way == RIGHT else -k, j)
        if joined:
            v = v + ri_in(way, k, j)
        ris[way, k - 1, j] = v.astype(BF16)
        ri_copy(way, k, j).start()

    ri_put(RIGHT, 4, 0, False)
    ri_put(LEFT, 4, 1, False)
    ri_put(RIGHT, 3, 1, False)
    ri_put(LEFT, 3, 0, False)

    lr = lrate[m]
    rate = jnp.exp(jnp.full((8, 128), lr, F32))[0:1, 0:1]
    flag = copyf[m]

    def middle_end(t):
        p = mate(t)
        g = dW[z, p] + rs_in(RIGHT, 0, p) + rs_in(LEFT, 0, p)
        nm[p] = (wq[z, p].astype(F32) - rate * g).astype(BF16)
        copy(nm.at[p], ym.at[p], y_s.at[p], y_r.at[p], after).start()

    middle_end(2)
    ri_put(RIGHT, 3, 0, True)
    ri_put(LEFT, 3, 1, True)
    middle_end(1)
    dh_in(RIGHT, 4)
    tot = dH[0]
    for b in range(1, Z):
        tot = tot + dH[b]
    dHg[q] = tot
    o_fit[0] = jnp.sum(tot[ACT : ACT + 1, :])

    def dh_mate(t):
        return copy(dHg.at[q], dHg.at[q], gp_s.at[DH, mate(t)], gp_r.at[DH, q], mate_id(t))

    for t in (2, 1, 3):
        dh_mate(t).start()
    for j in range(2):
        ri_put(RIGHT, 2, j, True)
        ri_put(LEFT, 2, j, True)
    middle_end(3)
    middle_end(0)
    for j in range(2):
        ri_put(RIGHT, 1, j, True)
        ri_put(LEFT, 1, j, True)

    def chosen(got, own):
        return jnp.where(jnp.full(own.shape, flag) == 1, got.astype(F32), own.astype(F32)).astype(BF16)

    def out_mate(p):
        return copy(nm.at[p], om.at[q], gp_s.at[OUT, p], gp_r.at[OUT, q], {"dp": z * Q + p})

    def middle_pick(t):
        p = mate(t)
        copy(nm.at[p], ym.at[p], y_s.at[p], y_r.at[p], after).wait()
        nm[p] = chosen(ym[p], nm[p])
        if t:
            out_mate(p).start()
        else:
            om[q] = nm[p]

    middle_pick(2)
    middle_pick(1)

    for t in (2, 1, 3):
        p = mate(t)
        copy(dHg.at[p], dHg.at[p], gp_s.at[DH, p], gp_r.at[DH, p], sib).wait_recv()
    tH[...] = jnp.transpose(dHg[z // 2])
    own_rows = pl.ds(pl.multiple_of(lax.rem(d, Z) * 64, 64), 64)
    nh[...] = (wh[z, h, c].astype(F32) - rate * tH[own_rows, 0:ACT]).astype(BF16)
    head_y = copy(nh, yh, y_s.at[5], y_r.at[5], after)
    head_y.start()
    middle_pick(3)
    middle_pick(0)
    for j in range(2):
        tin[j] = own_in(0, j) + ri_in(RIGHT, 0, j) + ri_in(LEFT, 0, j)
    xs[...] = tin[1 - h].astype(BF16)
    cross = copy(xs, xr, xp_s.at[2], xp_r.at[2], xpt)
    cross.start()
    head_y.wait_recv()
    o_head[...] = chosen(yh[...], nh[...])
    cross.wait_recv()
    ni[...] = (wi[z, h, c].astype(F32) - rate * (tin[h] + xr[...].astype(F32))).astype(BF16)
    in_y = copy(ni, yi, y_s.at[4], y_r.at[4], after)
    in_y.start()
    for t in (2, 1, 3):
        p = mate(t)
        copy(om.at[p], om.at[p], gp_s.at[OUT, p], gp_r.at[OUT, p], sib).wait_recv()
    for p in range(Q):
        o_mid[:, p * QC : (p + 1) * QC] = om[p]
    lr_before = lrate[lax.rem(m + POP - 1, POP)]
    pick = pert[m]
    o_rate[0] = jnp.where(flag == 1, lr_before, lr) + jnp.where(pick == 0, -0.2, jnp.where(pick == 1, 0.0, 0.2))
    in_y.wait_recv()
    o_in[...] = chosen(yi[...], ni[...])

    xwi.wait_send()
    xwh.wait_send()
    cross.wait_send()
    head_y.wait_send()
    in_y.wait_send()
    core_copy(wi, 0).wait_send()
    core_copy(wh, 1).wait_send()
    core_sum.wait_send()
    for t in (1, 2, 3):
        quarter(t).wait_send()
        sight(t).wait_send()
        raw_out(mate(t)).wait_send()
        gr_out(t).wait_send()
        dh_mate(t).wait_send()
        out_mate(mate(t)).wait_send()
    for k in range(1, K):
        for way in (RIGHT, LEFT):
            for j in range(2):
                for kind in (WI, WM, WH):
                    ag(kind, way, k, j).wait_send()
                ri_copy(way, k, j).wait_send()
            for p in range(Q):
                rs_copy(way, k, p).wait_send()
            dh_copy(way, k).wait_send()
    for kind in (WI, WM, WH):
        ag(kind, RIGHT, K, 0).wait_send()
        ag(kind, LEFT, K, 1).wait_send()
    ri_copy(RIGHT, K, 0).wait_send()
    ri_copy(LEFT, K, 1).wait_send()
    for j in range(2):
        rs_copy(RIGHT, K, j).wait_send()
        rs_copy(LEFT, K, 2 + j).wait_send()
    dh_copy(RIGHT, K).wait_send()


def local(observations, returns, actions, w_input, w_middle, w_head, log_rate, copy_from, perturb):
    hbm = pl.BlockSpec(memory_space=pltpu.HBM)
    vmem = pl.BlockSpec(memory_space=pltpu.VMEM)
    smem = pl.BlockSpec(memory_space=pltpu.SMEM)
    V = pltpu.VMEM
    S = pltpu.SemaphoreType.DMA
    out = pl.pallas_call(
        kernel,
        out_shape=(
            jax.ShapeDtypeStruct((8, D), BF16),
            jax.ShapeDtypeStruct((64, D), BF16),
            jax.ShapeDtypeStruct((64, ACT), BF16),
            jax.ShapeDtypeStruct((1,), F32),
            jax.ShapeDtypeStruct((1,), F32),
        ),
        in_specs=[hbm, vmem, vmem, hbm, hbm, hbm, smem, smem, smem],
        out_specs=(vmem, vmem, vmem, smem, smem),
        scratch_shapes=[
            V((Q, ROWS, OBS), BF16),
            V((OBS, D), BF16),
            V((Z, 2, 2, 8, D), BF16),
            V((Z, 2, 2, 64, ACT), BF16),
            V((Z, Q, 64, QC), BF16),
            V((D, OBS), BF16),
            V((QC, BK), BF16),
            V((D, D), BF16),
            V((D, D), BF16),
            V((QC, D), F32),
            V((QC, D), BF16),
            V((QC, D), BF16),
            V((QC, 128), F32),
            V((32, QC), BF16),
            V((Q, 24, ROWS), F32),
            V((Q, 24, ROWS), F32),
            V((Q, 32, ROWS), BF16),
            V((Z, Q, 64, QC), F32),
            V((2, K, Q, 64, QC), BF16),
            V((2, K, Q, 64, QC), BF16),
            V((Z, 2, 2, 8, D), F32),
            V((Z, 2, 8, D), BF16),
            V((Z, 2, 8, D), BF16),
            V((2, K, 2, 8, D), BF16),
            V((2, K, 2, 8, D), BF16),
            V((2, 8, D), F32),
            V((8, D), BF16),
            V((8, D), BF16),
            V((Z, 24, QC), F32),
            V((Q, 24, QC), F32),
            V((QC, 24), F32),
            V((Q, 64, QC), BF16),
            V((Q, 64, QC), BF16),
            V((Q, 64, QC), BF16),
            V((8, D), BF16),
            V((8, D), BF16),
            V((64, ACT), BF16),
            V((64, ACT), BF16),
            S((3, 2, K, 2)), S((3, 2, K, 2)),
            S((6, Q)), S((6, Q)),
            S((3,)), S((3,)),
            S((3,)), S((3,)),
            S((2, K)), S((2, K)),
            S((2, K, Q)), S((2, K, Q)),
            S((2, K, 2)), S((2, K, 2)),
            S((6,)), S((6,)),
            S((4,)),
        ],
        compiler_params=pltpu.CompilerParams(
            collective_id=0, has_side_effects=True, vmem_limit_bytes=64 * 1024 * 1024 - 65536
        ),
    )(observations[0], returns, actions, w_input[0], w_middle[0], w_head[0], log_rate, copy_from, perturb)
    return out[0][None], out[1][None], out[2][None], out[3], out[4]


def solution(mesh):
    in_specs = (
        P("pop", "dp", None),
        P("pop", "dp"),
        P("pop", "dp"),
        P("pop", "dp", None),
        P("pop", "dp", None),
        P("pop", "dp", None),
        P(),
        P(),
        P(),
    )
    out_specs = (
        P("pop", "dp", None),
        P("pop", "dp", None),
        P("pop", "dp", None),
        P("pop"),
        P("pop"),
    )
    return jax.shard_map(local, mesh=mesh, in_specs=in_specs, out_specs=out_specs, check_vma=False)
```

time: 390 us -> 148 us (0.38)
  waiting for transfers between devices: 294 us -> 0 us
  Pallas kernels: 0 us -> 138 us
  matrix products: 34.3 us -> 0 us
  starting transfers between devices: 22.7 us -> 0 us
  between operations: 19.1 us -> 4.09 us
  local copies, waits for them, and re-layouts: 11 us -> 5.08 us
  other arithmetic: 4.48 us -> 0 us
    all_gather x2 -> x0, waiting for transfers between devices: 180 us -> none  [the longest x1 94.5 us: local(): whole = lax.all_gather(own_middle, 'dp', axis=0, tiled=True)]
    pallas_call x0 -> x1, Pallas kernels: none -> 138 us  [local(): pl.pallas_call(kernel, out_shape=(jax.ShapeDtypeStruct((8, D), BF16), jax...]
    reduce_scatter x1 -> x0, waiting for transfers between devices: 76.2 us -> none  [local(): lax.psum_scatter(contract_rows(hidden1, grad_pre2).astype(jnp.bfloat16),...]
    dot_general x7 -> x0, matrix products: 34.3 us -> none  [the longest x3 20.5 us: contract_rows(): lax.dot_general(left, right, (((0,), (0,)), ((), ())), preferred_element_...]
    all_to_all x3 -> x0, waiting for transfers between devices: 31.9 us -> none  [the longest x2 24.3 us: sum_at_owner(): parts = lax.all_to_all(in_blocks(shard, dim, peers), axis, 0, 0, tiled=True)]
    all_to_all x3 -> x0, starting transfers between devices: 18.6 us -> none  [the longest x2 14 us: sum_at_owner(): parts = lax.all_to_all(in_blocks(shard, dim, peers), axis, 0, 0, tiled=True)]
    ppermute x3 -> x0, waiting for transfers between devices: 6.01 us -> none  [shifted(): return lax.ppermute(block, axis, route)]
    ppermute x3 -> x0, starting transfers between devices: 3.91 us -> none  [shifted(): return lax.ppermute(block, axis, route)]
  transfers between devices with their start and end apart: 9 -> 0, of which waited for: 7 -> 0; matrix products, arithmetic and copies ran while one was open for 7% -> 0% of each run, Pallas kernels for 0% -> 0%
where the time goes in v1:
time: 148 us; the launch traced here: 147 us
  Pallas kernels  138 us (93%)
  local copies, waits for them, and re-layouts  5.08 us (3%)
  between operations  4.09 us (3%)
    pallas_call x1, Pallas kernels, local(): pl.pallas_call(kernel, out_shape=(jax.ShapeDtypeStruct((8, D), BF16), jax...  138 us
    unnamed x6, local copies, waits for them, and re-layouts  5.08 us

profile of v1, /device:TPU:1, one launch (start us, length us, event | category | flops | bytes accessed | tf_op | source)
XLA Modules:
  0.0 146.7 jit_solution(10789062837233101514)
XLA Ops:
  0.6 1.4 copy.14
  2.0 137.6 %shard_map.128 = (bf16[8,2048]{1,0:T(8,128)(2,1)}, bf16[64,2048]{1,0:T(8,128)(2,1)}, bf16[64,18]{1,0:T(8,128)(2,1)}, f32[1]{0:T(128)}, f32[1]{0:T(128)}) custom-call(bf16[512,256]{1,0:T(8,128)(2,1)} %bitcast.8, f32[1,512]{1,0:T(1,128)} %ret.1, s32[1,512]{1,0:T(1,128)} %act.1, bf16[8,2048]{1,0:T(8,128)(2,1)} %bitcast.12, bf16[64,2048]{1,0:T(8,128)(2,1)} %bitcast.9, ...), custom_call_target="tpu_custom_call" | custom-call | tf_op jit(solution)/shard_map/pallas_call | solution.py:573
  139.6 0.0 copy-start
  139.6 1.4 copy.15
  141.0 0.0 copy-done
  141.0 0.6 copy.20
  141.6 1.7 %copy.21 = bf16[1,64,2048]{2,1,0:T(8,128)(2,1)} copy(bf16[1,64,2048]{2,1,0:T(8,128)(2,1)} %bitcast.7) | data formatting | bytes 524288
Async XLA Ops:
  139.6 1.4 copy-start

commit v2 on v1

v2 whole, which is shorter than its diff:
```python
import jax
import jax.numpy as jnp
from jax import lax
from jax.experimental import pallas as pl
from jax.experimental.pallas import tpu as pltpu
from jax.sharding import PartitionSpec as P

F32 = jnp.float32
BF16 = jnp.bfloat16
Z = 8
K = Z // 2
Q = 4
ROWS = 512
OBS = 256
D = 2048
QC = D // Q
BK = D // Z
ACT = 18
POP = 8
BATCH = ROWS * Z * Q
WM, WH = 0, 1
OB, QT, RAW, GR, DH, OUT = range(6)
RIGHT, LEFT = 0, 1
NEAR = (1, -1, 2, -2, 3, -3, K)


def nt(a, b):
    return lax.dot_general(a, b, (((1,), (1,)), ((), ())), preferred_element_type=F32)


def nn(a, b):
    return jnp.dot(a, b, preferred_element_type=F32)


def kernel(
    obs, ret, act, win, wmid, whead, lrate, copyf, pert,
    o_in, o_mid, o_head, o_rate, o_fit,
    ob, obT, wi, wh, wq, w1T, wT, dT, h1, s1, p2, h2, g2, whp, whq, whT,
    raw_s, raw_r, gr, dW, rss, rsb, dI, sib_s, sib_r, ris, rib, tin, xs, xr,
    xp, wp, dH, dHg, tH, nm, ym, om, ni, yi, nh, yh,
    ag_s, ag_r, wz_s, wz_r, wx_s, wx_r, gp_s, gp_r, xp_s, xp_r, sb_s, sb_r, dh_s, dh_r, rs_s, rs_r, ri_s, ri_r, y_s, y_r, loc,
):
    m = lax.axis_index("pop")
    d = lax.axis_index("dp")
    z = d // Q
    q = lax.rem(d, Q)
    h = q // 2
    c = lax.rem(q, 2)
    sib = {"dp": z * Q + h * 2 + (1 - c)}
    xpt = {"dp": z * Q + (1 - h) * 2 + c}
    side = [{"dp": lax.rem(z + 1, Z) * Q + q}, {"dp": lax.rem(z + Z - 1, Z) * Q + q}]
    after = {"pop": lax.rem(m + 1, POP)}
    m_after = lax.rem(m + 1, POP)
    m_before = lax.rem(m + POP - 1, POP)
    before = {"pop": m_before}

    def mate(t):
        return lax.rem(q + t, Q)

    def mate_id(t):
        return {"dp": z * Q + mate(t)}

    def at(off):
        return lax.rem(z + off + Z, Z)

    def column(off):
        return {"dp": at(off) * Q + q}

    def copy(src, dst, ss, rs, dev):
        return pltpu.make_async_remote_copy(
            src_ref=src, dst_ref=dst, send_sem=ss, recv_sem=rs, device_id=dev,
            device_id_type=pl.DeviceIdType.MESH,
        )

    fetch = [
        pltpu.make_async_copy(win, wi.at[z, h, c], loc.at[0]),
        pltpu.make_async_copy(wmid.at[:, pl.ds(pl.multiple_of(q * QC, QC), QC)], wq.at[z, q], loc.at[1]),
        pltpu.make_async_copy(whead, wh.at[z, h, c], loc.at[2]),
        pltpu.make_async_copy(obs, ob.at[q], loc.at[3]),
    ]
    for f in fetch:
        f.start()

    barrier = pltpu.get_barrier_semaphore()
    met = [mate_id(t) for t in (1, 2, 3)] + [after, before] + [column(off) for off in (2, -2, 1, -1)]
    for near in (m_after, m_before):
        met += [{"pop": near, "dp": z * Q + mate(t)} for t in (1, 2, 3)]
    for dev in met:
        pl.semaphore_signal(barrier, inc=1, device_id=dev, device_id_type=pl.DeviceIdType.MESH)
    pl.semaphore_wait(barrier, len(met))

    def win_out(off):
        i = NEAR.index(off)
        return copy(win, wi.at[z, h, c], wz_s.at[i], wz_r.at[i], column(off))

    def win_in(off):
        i = NEAR.index(off)
        ref = wi.at[at(-off), h, c]
        copy(ref, ref, wz_s.at[i], wz_r.at[i], xpt).wait_recv()

    def win_x(off):
        i = 7 if off == 0 else NEAR.index(off)
        ref = wi.at[at(-off), h, c]
        return copy(win if off == 0 else ref, ref, wx_s.at[i], wx_r.at[i], xpt)

    def win_x_in(off):
        i = 7 if off == 0 else NEAR.index(off)
        ref = wi.at[at(-off), 1 - h, c]
        copy(ref, ref, wx_s.at[i], wx_r.at[i], xpt).wait_recv()

    def win_on(step, off):
        i = NEAR.index(off)
        ref = wi.at[at(-2 * step), h, c]
        return copy(ref, ref, wz_s.at[i], wz_r.at[i], column(off - 2 * step))

    for off in (2, -2, 1, -1):
        win_out(off).start()
    win_x(0).start()
    prior = copy(win, wp, y_s.at[6], y_r.at[6], after)
    xwh = copy(whead, wh.at[z, h, c], xp_s.at[1], xp_r.at[1], xpt)

    def quarter(t):
        p = mate(t)
        return copy(
            wmid.at[:, pl.ds(pl.multiple_of(p * QC, QC), QC)], wq.at[z, q], gp_s.at[QT, p], gp_r.at[QT, q], mate_id(t)
        )

    x_mate = (1 - h) * 2 + c
    sight_x = copy(obs, ob.at[q], gp_s.at[OB, 0], gp_r.at[OB, q], xpt)
    sight_core = copy(obs, ob.at[q], gp_s.at[OB, 1], gp_r.at[OB, q], sib)
    sight_on = copy(ob.at[x_mate], ob.at[x_mate], gp_s.at[OB, 2], gp_r.at[OB, x_mate], sib)

    def quarter_in(p):
        copy(wq.at[z, p], wq.at[z, p], gp_s.at[QT, p], gp_r.at[QT, p], sib).wait_recv()

    for t in (1, 2, 3):
        quarter(t).start()
    xwh.start()
    sight_core.start()
    prior.start()
    p2[...] = jnp.zeros_like(p2)
    dT[...] = jnp.zeros_like(dT)

    def piece(kind, b, j):
        if kind == WM:
            return wq.at[b, pl.ds(2 * j, 2)]
        return wh.at[b, j, c]

    def ag(kind, way, k, j):
        b = at(1 - k) if way == RIGHT else at(k - 1)
        ref = piece(kind, b, j)
        return copy(ref, ref, ag_s.at[kind, way, k - 1, j], ag_r.at[kind, way, k - 1, j], side[way])

    def ag_in(kind, way, k, j):
        b = at(-k) if way == RIGHT else at(k)
        ref = piece(kind, b, j)
        copy(ref, ref, ag_s.at[kind, way, k - 1, j], ag_r.at[kind, way, k - 1, j], side[way]).wait_recv()

    def put(kinds, k, j):
        for kind in kinds:
            for way in (RIGHT, LEFT):
                ag(kind, way, k, j).start()

    def take(kinds, k, j):
        for kind in kinds:
            for way in (RIGHT, LEFT):
                ag_in(kind, way, k, j)

    def take_last(kinds, k):
        for kind in kinds:
            ag_in(kind, RIGHT, k, 0)
            ag_in(kind, LEFT, k, 1)

    def put_last(kinds):
        for kind in kinds:
            ag(kind, RIGHT, K, 0).start()
            ag(kind, LEFT, K, 1).start()

    MID = (WM, WH)

    def core_copy(off, i):
        b = at(-off)
        return copy(wi.at[b, :, c], wi.at[b, :, c], sb_s.at[i], sb_r.at[i], sib)

    def core_in(off, i):
        b = at(-off)
        copy(wi.at[b, :, 1 - c], wi.at[b, :, 1 - c], sb_s.at[i], sb_r.at[i], sib).wait_recv()

    core_off = (0,) + NEAR
    head_core = copy(wh.at[:, :, c], wh.at[:, :, c], sb_s.at[9], sb_r.at[9], sib)

    def head_core_in():
        copy(wh.at[:, :, 1 - c], wh.at[:, :, 1 - c], sb_s.at[9], sb_r.at[9], sib).wait_recv()

    for off in NEAR[:2]:
        win_in(off)
        win_x(off).start()
    fetch[1].wait()
    fetch[2].wait()
    quarter_in(h * 2 + (1 - c))
    put(MID, 1, h)
    for off in NEAR[2:4]:
        win_in(off)
        win_on(off // 2, 3 * off // 2).start()
        if off > 0:
            win_on(1, K).start()
        win_x(off).start()
    for off in NEAR[4:]:
        win_in(off)
        win_x(off).start()
    sight_x.start()
    fetch[0].wait()
    quarter_in((1 - h) * 2)
    quarter_in((1 - h) * 2 + 1)
    xwh.wait_recv()
    put(MID, 1, 1 - h)
    for i, off in enumerate(core_off[:3]):
        win_x_in(off)
        core_copy(off, i).start()
    take(MID, 1, h)
    put(MID, 2, h)
    for i, off in enumerate(core_off[3:]):
        win_x_in(off)
        core_copy(off, 3 + i).start()
    def obs_in(p):
        copy(ob.at[p], ob.at[p], gp_s.at[OB, 0], gp_r.at[OB, p], sib).wait_recv()

    fetch[3].wait()
    obs_in(h * 2 + (1 - c))

    def turn(p):
        cols = pl.ds(pl.multiple_of(p * ROWS, ROWS), ROWS)
        obT[:, cols] = jnp.transpose(ob[p].astype(F32)).astype(BF16)

    def group_at(i):
        return (h + i // 2 * (1 - 2 * h)) * 2 + c + i % 2 * (1 - 2 * c)

    def turn_by(i, _):
        turn(group_at(i))
        return 0

    lax.fori_loop(0, 2, turn_by, 0)
    take(MID, 1, 1 - h)
    put(MID, 2, 1 - h)
    for i in range(8):
        core_in(core_off[i], i)

    def turn_in(i, _):
        cols = pl.ds(pl.multiple_of(i * 256, 256), 256)
        x = wi[:, :, :, :, cols].astype(F32).reshape(OBS, 256)
        w1T[cols, :] = (0.5 * jnp.transpose(x)).astype(BF16)
        return 0

    lax.fori_loop(0, D // 256, turn_in, 0)

    def block_of(i):
        return at(((i + 1) // 2) * (2 * lax.rem(i + 1, 2) - 1))

    def first(i, p):
        feats = pl.ds(pl.multiple_of(block_of(i) * BK, BK), BK)
        rows = slice(p * ROWS, (p + 1) * ROWS)
        u = nn(w1T[feats, :], obT[:, rows])
        t = jnp.tanh(u)
        a = 1.0 + t
        hid = u * a
        h1[feats, rows] = hid.astype(BF16)
        s1[feats, rows] = (a + hid * (1.0 - t)).astype(BF16)

    def turn_w(i):
        wT[...] = (0.5 * jnp.transpose(wq[block_of(i)].astype(F32).reshape(BK, QC))).astype(BF16)

    def second(i, p):
        feats = pl.ds(pl.multiple_of(block_of(i) * BK, BK), BK)
        rows = slice(p * ROWS, (p + 1) * ROWS)
        p2[:, rows] += nn(wT[...], h1[feats, rows])

    def first_by(i, _):
        @pl.when(i == 0)
        def _():
            with jax.named_scope("wait0"):
                take(MID, 2, h)
                put(MID, 3, h)

        @pl.when(i == 2)
        def _():
            with jax.named_scope("wait2"):
                take(MID, 2, 1 - h)
                put(MID, 3, 1 - h)

        @pl.when(i == 6)
        def _():
            with jax.named_scope("wait6"):
                take_last(MID, 3)
                put_last(MID)

        for p in range(Q):
            first(i, p)
        return 0

    def second_by(i, _):
        @pl.when(i == 5)
        def _():
            with jax.named_scope("wait5s"):
                for kind in MID:
                    ag_in(kind, RIGHT, 3, 1)
                    ag_in(kind, LEFT, 3, 0)

        turn_w(i)
        for p in range(Q):
            second(i, p)
        return 0

    obs_in(x_mate)
    sight_on.start()
    turn_by(2, 0)
    obs_in((1 - h) * 2 + (1 - c))
    turn_by(3, 0)
    lax.fori_loop(0, Z, first_by, 0)
    lax.fori_loop(0, Z - 1, second_by, 0)
    take_last(MID, K)
    head_core.start()
    turn_w(Z - 1)
    for p in range(Q):
        second(Z - 1, p)

    head_core_in()
    whp[...] = jnp.zeros_like(whp)
    for b in range(2):
        for i in range(Q):
            lanes = slice((b * Q + i) * 64, (b * Q + i + 1) * 64)
            whp[0:ACT, lanes] = wh[2 * q + b, i // 2, i % 2].astype(F32)
    whT[...] = whp[0:32, :].astype(BF16)
    whq[...] = jnp.transpose(whp[...]).astype(BF16)

    def raw_out(p):
        return copy(raw_s.at[p], raw_r.at[q], gp_s.at[RAW, p], gp_r.at[RAW, q], {"dp": z * Q + p})

    for t in (2, 1, 3, 0):
        p = mate(t)
        rows = pl.ds(pl.multiple_of(p * ROWS, ROWS), ROWS)

        def forward2(i, _):
            cols = pl.ds(pl.multiple_of(p * ROWS + i * 128, 128), 128)
            u = p2[:, cols]
            h2[:, cols] = (u + u * jnp.tanh(u)).astype(BF16)
            return 0

        lax.fori_loop(0, 4, forward2, 0)
        raw_s[p] = nn(whT[...], h2[:, rows])[0:24, :]
        if t:
            raw_out(p).start()
    def slope2(i, _):
        cols = pl.ds(pl.multiple_of(i * 128, 128), 128)
        u = p2[:, cols]
        t = jnp.tanh(u)
        a = 1.0 + t
        p2[:, cols] = a + u * a * (1.0 - t)
        return 0

    lax.fori_loop(0, D // 128, slope2, 0)
    raw = raw_s[q]
    for t in (2, 1, 3):
        p = mate(t)
        copy(raw_r.at[p], raw_r.at[p], gp_s.at[RAW, p], gp_r.at[RAW, p], sib).wait_recv()
        raw = raw + raw_r[p]
    at_act = lax.broadcasted_iota(jnp.int32, raw.shape, 0)
    squash = jnp.tanh(raw * 0.5)
    logits = 2.0 * squash
    e = jnp.where(at_act < ACT, jnp.exp(logits), 0.0)
    total = jnp.sum(e, axis=0, keepdims=True)
    logp = logits - jnp.log(total)
    onehot = jnp.where(at_act == act[...], 1.0, 0.0)
    gains = ret[...] * (1.0 / BATCH)
    term = gains * jnp.sum(logp * onehot, axis=0, keepdims=True)
    grad = -gains * (onehot - e / total) * (1.0 - squash * squash)
    high = term.astype(BF16).astype(F32)
    low = term - high
    grad = jnp.where(at_act < ACT, grad, jnp.where(at_act == ACT, high, jnp.where(at_act == ACT + 1, low, 0.0)))
    gr[q] = jnp.concatenate([grad, jnp.zeros((8, ROWS), F32)], axis=0).astype(BF16)

    def gr_out(t):
        return copy(gr.at[q], gr.at[q], gp_s.at[GR, mate(t)], gp_r.at[GR, q], mate_id(t))

    for t in (2, 1, 3):
        gr_out(t).start()
    wb = (0.5 * whq[:, 0:32].astype(F32)).astype(BF16)

    def grad2(i):
        p = group_at(i)
        if i:
            copy(gr.at[p], gr.at[p], gp_s.at[GR, p], gp_r.at[GR, p], sib).wait_recv()
        rows = pl.ds(pl.multiple_of(p * ROWS, ROWS), ROWS)
        g2[:, rows] = (nn(wb, gr[p]) * p2[:, rows]).astype(BF16)

    def back(i, _):
        p = group_at(i // 2)
        rows = pl.ds(pl.multiple_of(p * ROWS, ROWS), ROWS)
        half = lax.rem(i, 2)
        feats = pl.ds(pl.multiple_of(half * (D // 2), D // 2), D // 2)
        w = wq[pl.ds(half * (Z // 2), Z // 2)].reshape(D // 2, QC)
        g = (nn(w, g2[:, rows]) * s1[feats, rows].astype(F32)).astype(BF16)
        dT[feats, :] += nn(g, ob[p])
        return 0

    grad2(0)
    lax.fori_loop(0, 2, back, 0)
    grad2(1)
    grad2(2)
    grad2(3)

    def middle(i, _):
        one = at(K + i)
        two = at(K - 1 - i)
        at_one = pl.ds(pl.multiple_of(one * BK, BK), BK)
        at_two = pl.ds(pl.multiple_of(two * BK, BK), BK)
        both = nt(jnp.concatenate([h1[at_one, :], h1[at_two, :]], axis=0), g2[...])
        dW[one] = both[0:BK].reshape(Q, BK // Q, QC)
        dW[two] = both[BK:].reshape(Q, BK // Q, QC)
        return 0

    def rs_copy(way, k, p):
        return copy(
            rss.at[way, k - 1, p], rsb.at[way, k - 1, p], rs_s.at[way, k - 1, p], rs_r.at[way, k - 1, p], side[way]
        )

    def rs_in(way, k, p):
        copy(rsb.at[way, k, p], rsb.at[way, k, p], rs_s.at[way, k, p], rs_r.at[way, k, p], side[way]).wait_recv()
        return rsb[way, k, p].astype(F32)

    def rs_put(way, k, p, joined):
        v = dW[at(k if way == RIGHT else -k), p]
        if joined:
            v = v + rs_in(way, k, p)
        rss[way, k - 1, p] = v.astype(BF16)
        rs_copy(way, k, p).start()

    def rs_open(j, _):
        rs_put(RIGHT, K, j, False)
        rs_put(LEFT, K, 2 + j, False)
        return 0

    def rs_open2(j, _):
        rs_put(RIGHT, K - 1, 2 + j, False)
        rs_put(LEFT, K - 1, j, False)
        return 0

    def middle_open(i, _):
        middle(i, 0)

        @pl.when(i == 0)
        def _():
            lax.fori_loop(0, 2, rs_open, 0)

        return 0

    lax.fori_loop(0, 2, middle_open, 0)
    lax.fori_loop(0, 2, rs_open2, 0)

    acc = jnp.zeros((32, QC), F32)
    fit = jnp.zeros((1, ROWS), F32)
    for p in range(Q):
        acc = acc + nt(gr[p], h2[:, p * ROWS : (p + 1) * ROWS])
        x = gr[p].astype(F32)
        fit = fit + x[ACT : ACT + 1, :] + x[ACT + 1 : ACT + 2, :]
    at_head = lax.broadcasted_iota(jnp.int32, (24, QC), 0)
    fit_high = fit.astype(BF16).astype(F32)
    packed = jnp.where(at_head == ACT, fit_high, jnp.where(at_head == ACT + 1, fit - fit_high, acc[0:24, :]))
    dH[z] = packed.astype(BF16)

    def dh_out(off):
        i = NEAR.index(off)
        return copy(dH.at[z], dH.at[z], dh_s.at[i], dh_r.at[i], column(off))

    def dh_on(step, off):
        i = NEAR.index(off)
        ref = dH.at[at(-2 * step)]
        return copy(ref, ref, dh_s.at[i], dh_r.at[i], column(off - 2 * step))

    def dh_in(off):
        i = NEAR.index(off)
        ref = dH.at[at(-off)]
        copy(ref, ref, dh_s.at[i], dh_r.at[i], sib).wait_recv()

    for off in (2, -2, 1, -1):
        dh_out(off).start()

    def join3(j, _):
        rs_put(RIGHT, K - 1, j, True)
        rs_put(LEFT, K - 1, 2 + j, True)
        return 0

    def join2(j, _):
        rs_put(RIGHT, 2, lax.rem(2 + j, Q), True)
        rs_put(LEFT, 2, j, True)
        return 0

    lax.fori_loop(2, 4, back, 0)
    lax.fori_loop(0, 2, join3, 0)
    lax.fori_loop(4, 8, back, 0)

    def turn_back(i, _):
        feats = pl.ds(pl.multiple_of(i * 256, 256), 256)
        x = 0.5 * jnp.transpose(dT[feats, :])
        dI[:, :, :, :, feats] = x.reshape(Z, 2, 2, 8, 256)
        return 0

    dh_in(2)
    dh_on(1, 3).start()
    dh_on(1, K).start()
    dh_in(-2)
    dh_on(-1, -3).start()
    lax.fori_loop(0, Z, turn_back, 0)

    for b in range(Z):
        for j in range(2):
            sib_s[b, j] = dI[b, j, 1 - c].astype(BF16)
    core_sum = copy(sib_s, sib_r, sb_s.at[8], sb_r.at[8], sib)
    core_sum.start()
    lax.fori_loop(2, 4, middle, 0)
    core_sum.wait_recv()

    def own_in(off, j):
        b = at(off)
        return dI[b, j, c] + sib_r[b, j].astype(F32)

    def ri_copy(way, k, j):
        return copy(
            ris.at[way, k - 1, j], rib.at[way, k - 1, j], ri_s.at[way, k - 1, j], ri_r.at[way, k - 1, j], side[way]
        )

    def ri_in(way, k, j):
        copy(rib.at[way, k, j], rib.at[way, k, j], ri_s.at[way, k, j], ri_r.at[way, k, j], side[way]).wait_recv()
        return rib[way, k, j].astype(F32)

    def ri_put(way, k, j, joined):
        v = own_in(k if way == RIGHT else -k, j)
        if joined:
            v = v + ri_in(way, k, j)
        ris[way, k - 1, j] = v.astype(BF16)
        ri_copy(way, k, j).start()

    ri_put(RIGHT, 4, 0, False)
    ri_put(LEFT, 4, 1, False)
    ri_put(RIGHT, 3, 1, False)
    ri_put(LEFT, 3, 0, False)

    lr = lrate[m]
    lr_before = lrate[m_before]
    rate = jnp.exp(jnp.full((8, 128), lr, F32))[0:1, 0:1]
    rate_before = jnp.exp(jnp.full((8, 128), lr_before, F32))[0:1, 0:1]
    flag = copyf[m]

    def next_out(p):
        return copy(nm.at[p], ym.at[q], y_s.at[p], y_r.at[q], {"pop": m_after, "dp": z * Q + p})

    def out_mate(p):
        return copy(nm.at[p], om.at[q], gp_s.at[OUT, p], gp_r.at[OUT, q], {"dp": z * Q + p})

    def middle_end(p):
        g = dW[z, p] + rs_in(RIGHT, 0, p) + rs_in(LEFT, 0, p)
        nm[p] = (wq[z, p].astype(F32) - rate * g).astype(BF16)
        next_out(p).start()

        @pl.when(p != q)
        def _():
            out_mate(p).start()

    def ones(j, _):
        rs_put(RIGHT, 1, lax.rem(2 + j, Q), True)
        rs_put(LEFT, 1, j, True)
        return 0

    lax.fori_loop(0, 2, join2, 0)
    ri_put(RIGHT, 3, 0, True)
    ri_put(LEFT, 3, 1, True)
    lax.fori_loop(2, 4, join2, 0)
    for off in (1, -1, 3, -3, K):
        dh_in(off)
    tot = dH[0].astype(F32)
    for b in range(1, Z):
        tot = tot + dH[b].astype(F32)
    dHg[q] = tot
    o_fit[0] = jnp.sum(tot[ACT : ACT + 2, :])

    def dh_mate(t):
        return copy(dHg.at[q], dHg.at[q], gp_s.at[DH, mate(t)], gp_r.at[DH, q], mate_id(t))

    for t in (2, 1, 3):
        dh_mate(t).start()

    lax.fori_loop(0, 2, ones, 0)
    for j in range(2):
        ri_put(RIGHT, 2, j, True)
        ri_put(LEFT, 2, j, True)
    lax.fori_loop(2, 4, ones, 0)
    for t in (2, 1, 3):
        p = mate(t)
        copy(dHg.at[p], dHg.at[p], gp_s.at[DH, p], gp_r.at[DH, p], sib).wait_recv()
    tH[...] = jnp.transpose(dHg[z // 2])
    own_rows = pl.ds(pl.multiple_of(lax.rem(d, Z) * 64, 64), 64)
    nh[...] = (wh[z, h, c].astype(F32) - rate * jnp.transpose(tH[own_rows, :])[0:ACT, :]).astype(BF16)
    head_y = copy(nh, yh, y_s.at[5], y_r.at[5], after)
    head_y.start()
    middle_end(0)
    middle_end(2)
    for j in range(2):
        ri_put(RIGHT, 1, j, True)
        ri_put(LEFT, 1, j, True)
    middle_end(1)
    middle_end(3)
    def chosen(got, own):
        return jnp.where(jnp.full(own.shape, flag) == 1, got.astype(F32), own.astype(F32)).astype(BF16)

    for j in range(2):
        tin[j] = own_in(0, j) + ri_in(RIGHT, 0, j) + ri_in(LEFT, 0, j)
    xs[...] = tin[1 - h].astype(BF16)
    cross = copy(xs, xr, xp_s.at[2], xp_r.at[2], xpt)
    cross.start()
    cross_y = copy(xs, xp, xp_s.at[0], xp_r.at[0], {"pop": m_after, "dp": xpt["dp"]})
    cross_y.start()
    ni[...] = tin[h].astype(BF16)
    in_y = copy(ni, yi, y_s.at[4], y_r.at[4], after)
    in_y.start()
    head_y.wait_recv()
    o_head[...] = chosen(yh[...], nh[...])
    for t in (0, 1, 2, 3):
        p = mate(t)
        own = nm.at[p] if t == 0 else om.at[p]
        if t:
            copy(own, own, gp_s.at[OUT, p], gp_r.at[OUT, p], sib).wait_recv()
        copy(ym.at[p], ym.at[p], y_s.at[p], y_r.at[p], after).wait_recv()
        o_mid[:, pl.ds(pl.multiple_of(p * QC, QC), QC)] = chosen(ym[p], own[...])
    pick = pert[m]
    o_rate[0] = jnp.where(flag == 1, lr_before, lr) + jnp.where(pick == 0, -0.2, jnp.where(pick == 1, 0.0, 0.2))
    prior.wait_recv()
    cross.wait_recv()
    cross_y.wait_recv()
    in_y.wait_recv()
    new = wi[z, h, c].astype(F32) - rate * (tin[h] + xr[...].astype(F32))
    new_before = wp[...].astype(F32) - rate_before * (yi[...].astype(F32) + xp[...].astype(F32))
    o_in[...] = chosen(new_before, new)

    for off in NEAR:
        if off in (1, -1, 2, -2):
            win_out(off).wait_send()
        else:
            win_on(1 if off > 0 else -1, off).wait_send()
        win_x(off).wait_send()
    win_x(0).wait_send()
    prior.wait_send()
    cross_y.wait_send()
    for p in range(Q):
        next_out(p).wait_send()
    xwh.wait_send()
    cross.wait_send()
    head_y.wait_send()
    in_y.wait_send()
    for i in range(8):
        core_copy(core_off[i], i).wait_send()
    head_core.wait_send()
    sight_x.wait_send()
    sight_core.wait_send()
    sight_on.wait_send()
    core_sum.wait_send()
    for t in (1, 2, 3):
        quarter(t).wait_send()
        raw_out(mate(t)).wait_send()
        gr_out(t).wait_send()
        dh_mate(t).wait_send()
        out_mate(mate(t)).wait_send()
    for k in range(1, K):
        for way in (RIGHT, LEFT):
            for j in range(2):
                for kind in MID:
                    ag(kind, way, k, j).wait_send()
                ri_copy(way, k, j).wait_send()
            for p in range(Q):
                rs_copy(way, k, p).wait_send()
    for kind in MID:
        ag(kind, RIGHT, K, 0).wait_send()
        ag(kind, LEFT, K, 1).wait_send()
    ri_copy(RIGHT, K, 0).wait_send()
    ri_copy(LEFT, K, 1).wait_send()
    for j in range(2):
        rs_copy(RIGHT, K, j).wait_send()
        rs_copy(LEFT, K, 2 + j).wait_send()
    for off in (1, -1, 2, -2):
        dh_out(off).wait_send()
    for off in (3, -3, K):
        dh_on(1 if off > 0 else -1, off).wait_send()


def local(observations, returns, actions, w_input, w_middle, w_head, log_rate, copy_from, perturb):
    hbm = pl.BlockSpec(memory_space=pltpu.HBM)
    vmem = pl.BlockSpec(memory_space=pltpu.VMEM)
    smem = pl.BlockSpec(memory_space=pltpu.SMEM)
    V = pltpu.VMEM
    S = pltpu.SemaphoreType.DMA
    out = pl.pallas_call(
        kernel,
        out_shape=(
            jax.ShapeDtypeStruct((8, D), BF16),
            jax.ShapeDtypeStruct((64, D), BF16),
            jax.ShapeDtypeStruct((ACT, 64), BF16),
            jax.ShapeDtypeStruct((1,), F32),
            jax.ShapeDtypeStruct((1,), F32),
        ),
        in_specs=[hbm, vmem, vmem, hbm, hbm, hbm, smem, smem, smem],
        out_specs=(vmem, vmem, vmem, smem, smem),
        scratch_shapes=[
            V((Q, ROWS, OBS), BF16),
            V((OBS, D), BF16),
            V((Z, 2, 2, 8, D), BF16),
            V((Z, 2, 2, ACT, 64), BF16),
            V((Z, Q, 64, QC), BF16),
            V((D, OBS), BF16),
            V((QC, BK), BF16),
            V((D, OBS), F32),
            V((D, D), BF16),
            V((D, D), BF16),
            V((QC, D), F32),
            V((QC, D), BF16),
            V((QC, D), BF16),
            V((128, QC), F32),
            V((QC, 128), BF16),
            V((32, QC), BF16),
            V((Q, 24, ROWS), F32),
            V((Q, 24, ROWS), F32),
            V((Q, 32, ROWS), BF16),
            V((Z, Q, 64, QC), F32),
            V((2, K, Q, 64, QC), BF16),
            V((2, K, Q, 64, QC), BF16),
            V((Z, 2, 2, 8, D), F32),
            V((Z, 2, 8, D), BF16),
            V((Z, 2, 8, D), BF16),
            V((2, K, 2, 8, D), BF16),
            V((2, K, 2, 8, D), BF16),
            V((2, 8, D), F32),
            V((8, D), BF16),
            V((8, D), BF16),
            V((8, D), BF16),
            V((8, D), BF16),
            V((Z, 24, QC), BF16),
            V((Q, 24, QC), F32),
            V((QC, 24), F32),
            V((Q, 64, QC), BF16),
            V((Q, 64, QC), BF16),
            V((Q, 64, QC), BF16),
            V((8, D), BF16),
            V((8, D), BF16),
            V((ACT, 64), BF16),
            V((ACT, 64), BF16),
            S((2, 2, K, 2)), S((2, 2, K, 2)),
            S((7,)), S((7,)),
            S((8,)), S((8,)),
            S((6, Q)), S((6, Q)),
            S((3,)), S((3,)),
            S((10,)), S((10,)),
            S((7,)), S((7,)),
            S((2, K, Q)), S((2, K, Q)),
            S((2, K, 2)), S((2, K, 2)),
            S((7,)), S((7,)),
            S((4,)),
        ],
        compiler_params=pltpu.CompilerParams(
            collective_id=0, has_side_effects=True, vmem_limit_bytes=64 * 1024 * 1024 - 65536
        ),
    )(observations[0], returns, actions, w_input[0], w_middle[0], w_head[0].T, log_rate, copy_from, perturb)
    return out[0][None], out[1][None], out[2].T[None], out[3], out[4]


def solution(mesh):
    in_specs = (
        P("pop", "dp", None),
        P("pop", "dp"),
        P("pop", "dp"),
        P("pop", "dp", None),
        P("pop", "dp", None),
        P("pop", "dp", None),
        P(),
        P(),
        P(),
    )
    out_specs = (
        P("pop", "dp", None),
        P("pop", "dp", None),
        P("pop", "dp", None),
        P("pop"),
        P("pop"),
    )
    return jax.shard_map(local, mesh=mesh, in_specs=in_specs, out_specs=out_specs, check_vma=False)
```

time: 148 us -> 107 us (0.72)
  Pallas kernels: 138 us -> 99.4 us
    pallas_call x1, Pallas kernels: 138 us -> 99.4 us  [local(): pl.pallas_call(kernel, out_shape=(jax.ShapeDtypeStruct((8, D), BF16), jax...]
    unnamed x6 -> x5, local copies, waits for them, and re-layouts: 5.08 us -> 3.65 us
where the time goes in v2:
time: 107 us
  Pallas kernels  99.4 us (93%)
  between operations  4.09 us (4%)
  local copies, waits for them, and re-layouts  3.65 us (3%)
    pallas_call x1, Pallas kernels, local(): pl.pallas_call(kernel, out_shape=(jax.ShapeDtypeStruct((8, D), BF16), jax...  99.4 us
    unnamed x5, local copies, waits for them, and re-layouts  3.65 us

profile of v2, /device:TPU:1, one launch (start us, length us, event | category | flops | bytes accessed | tf_op | source)
XLA Modules:
  0.0 107.2 jit_solution(2507480649945455558)
XLA Ops:
  0.6 99.4 %shard_map.128 = (bf16[8,2048]{1,0:T(8,128)(2,1)}, bf16[64,2048]{1,0:T(8,128)(2,1)}, bf16[18,64]{1,0:T(8,128)(2,1)}, f32[1]{0:T(128)}, f32[1]{0:T(128)}) custom-call(bf16[512,256]{1,0:T(8,128)(2,1)} %bitcast.12, f32[1,512]{1,0:T(1,128)} %ret.1, s32[1,512]{1,0:T(1,128)} %act.1, bf16[8,2048]{1,0:T(8,128)(2,1)} %bitcast.15, bf16[64,2048]{1,0:T(8,128)(2,1)} %bitcast.13, ...), custom_call_target="tpu_custom_call" | custom-call | tf_op jit(solution)/shard_map/pallas_call | solution.py:699
  100.1 1.4 %copy.19 = bf16[1,8,2048]{2,1,0:T(8,128)(2,1)} copy(bf16[1,8,2048]{2,1,0:T(8,128)(2,1)} %bitcast.14) | data formatting | bytes 65536
  101.5 0.0 copy-start
  101.5 1.7 %copy.20 = bf16[1,64,2048]{2,1,0:T(8,128)(2,1)} copy(bf16[1,64,2048]{2,1,0:T(8,128)(2,1)} %bitcast.11) | data formatting | bytes 524288
  103.1 0.0 copy-done
  103.2 0.6 copy.21
Async XLA Ops:
  101.5 1.7 %copy-start = (bf16[18,64]{1,0:T(8,128)(2,1)S(1)}, bf16[18,64]{1,0:T(8,128)(2,1)}, u32[]{:S(2)}) copy-start(bf16[18,64]{1,0:T(8,128)(2,1)} %get-tuple-element.12) | copy-start | bytes 6916

commit v3 on v2

--- a/solution.py
+++ b/solution.py
@@ -192,54 +192,52 @@
     def head_core_in():
         copy(wh.at[:, :, 1 - c], wh.at[:, :, 1 - c], sb_s.at[9], sb_r.at[9], sib).wait_recv()
 
+    def obs_in(p):
+        copy(ob.at[p], ob.at[p], gp_s.at[OB, 0], gp_r.at[OB, p], sib).wait_recv()
+
+    def group_at(i):
+        return (h + i // 2 * (1 - 2 * h)) * 2 + c + i % 2 * (1 - 2 * c)
+
+    def turn_by(i, _):
+        p = group_at(i)
+        cols = pl.ds(pl.multiple_of(p * ROWS, ROWS), ROWS)
+        obT[:, cols] = jnp.transpose(ob[p].astype(F32)).astype(BF16)
+        return 0
+
     for off in NEAR[:2]:
         win_in(off)
         win_x(off).start()
-    fetch[1].wait()
-    fetch[2].wait()
-    quarter_in(h * 2 + (1 - c))
-    put(MID, 1, h)
     for off in NEAR[2:4]:
         win_in(off)
         win_on(off // 2, 3 * off // 2).start()
         if off > 0:
             win_on(1, K).start()
         win_x(off).start()
+    fetch[1].wait()
+    fetch[2].wait()
+    quarter_in(h * 2 + (1 - c))
+    put(MID, 1, h)
+    quarter_in((1 - h) * 2)
+    quarter_in((1 - h) * 2 + 1)
+    xwh.wait_recv()
+    put(MID, 1, 1 - h)
+    fetch[3].wait()
+    turn_by(0, 0)
+    obs_in(h * 2 + (1 - c))
+    turn_by(1, 0)
     for off in NEAR[4:]:
         win_in(off)
         win_x(off).start()
     sight_x.start()
     fetch[0].wait()
-    quarter_in((1 - h) * 2)
-    quarter_in((1 - h) * 2 + 1)
-    xwh.wait_recv()
-    put(MID, 1, 1 - h)
-    for i, off in enumerate(core_off[:3]):
+    for i, off in enumerate(core_off[:5]):
         win_x_in(off)
         core_copy(off, i).start()
     take(MID, 1, h)
     put(MID, 2, h)
-    for i, off in enumerate(core_off[3:]):
+    for i, off in enumerate(core_off[5:]):
         win_x_in(off)
-        core_copy(off, 3 + i).start()
-    def obs_in(p):
-        copy(ob.at[p], ob.at[p], gp_s.at[OB, 0], gp_r.at[OB, p], sib).wait_recv()
-
-    fetch[3].wait()
-    obs_in(h * 2 + (1 - c))
-
-    def turn(p):
-        cols = pl.ds(pl.multiple_of(p * ROWS, ROWS), ROWS)
-        obT[:, cols] = jnp.transpose(ob[p].astype(F32)).astype(BF16)
-
-    def group_at(i):
-        return (h + i // 2 * (1 - 2 * h)) * 2 + c + i % 2 * (1 - 2 * c)
-
-    def turn_by(i, _):
-        turn(group_at(i))
-        return 0
-
-    lax.fori_loop(0, 2, turn_by, 0)
+        core_copy(off, 5 + i).start()
     take(MID, 1, 1 - h)
     put(MID, 2, 1 - h)
     for i in range(8):
@@ -257,8 +255,8 @@
         return at(((i + 1) // 2) * (2 * lax.rem(i + 1, 2) - 1))
 
     def first(i, p):
-        feats = pl.ds(pl.multiple_of(block_of(i) * BK, BK), BK)
-        rows = slice(p * ROWS, (p + 1) * ROWS)
+        feats = pl.ds(pl.multiple_of(i * BK, BK), BK)
+        rows = pl.ds(pl.multiple_of(p * ROWS, ROWS), ROWS)
         u = nn(w1T[feats, :], obT[:, rows])
         t = jnp.tanh(u)
         a = 1.0 + t
@@ -266,26 +264,38 @@
         h1[feats, rows] = hid.astype(BF16)
         s1[feats, rows] = (a + hid * (1.0 - t)).astype(BF16)
 
+    def block_rows(i):
+        return pl.ds(pl.multiple_of(block_of(i) * BK, BK), BK)
+
     def turn_w(i):
-        wT[...] = (0.5 * jnp.transpose(wq[block_of(i)].astype(F32).reshape(BK, QC))).astype(BF16)
-
-    def second(i, p):
-        feats = pl.ds(pl.multiple_of(block_of(i) * BK, BK), BK)
-        rows = slice(p * ROWS, (p + 1) * ROWS)
-        p2[:, rows] += nn(wT[...], h1[feats, rows])
+        for b in range(2):
+            x = wq[block_of(2 * i + b)].astype(F32).reshape(BK, QC)
+            wT[b] = (0.5 * jnp.transpose(x)).astype(BF16)
+
+    def second(i, rows):
+        p2[:, rows] += nn(wT[0], h1[block_rows(2 * i), rows]) + nn(wT[1], h1[block_rows(2 * i + 1), rows])
 
     def first_by(i, _):
-        @pl.when(i == 0)
+        @pl.when(i == 1)
         def _():
-            with jax.named_scope("wait0"):
+            with jax.named_scope("wait1"):
                 take(MID, 2, h)
                 put(MID, 3, h)
 
-        @pl.when(i == 2)
+        @pl.when(i == 3)
         def _():
-            with jax.named_scope("wait2"):
+            with jax.named_scope("wait3"):
+                obs_in(x_mate)
+                sight_on.start()
+                turn_by(2, 0)
+
+        @pl.when(i == 4)
+        def _():
+            with jax.named_scope("wait4"):
                 take(MID, 2, 1 - h)
                 put(MID, 3, 1 - h)
+                obs_in((1 - h) * 2 + (1 - c))
+                turn_by(3, 0)
 
         @pl.when(i == 6)
         def _():
@@ -293,35 +303,29 @@
                 take_last(MID, 3)
                 put_last(MID)
 
-        for p in range(Q):
-            first(i, p)
+        for b in range(2):
+            for p in range(2):
+                first(i % K * 2 + b, group_at(i // K * 2 + p))
         return 0
 
     def second_by(i, _):
-        @pl.when(i == 5)
+        @pl.when(i == 2)
         def _():
-            with jax.named_scope("wait5s"):
+            with jax.named_scope("wait2s"):
                 for kind in MID:
                     ag_in(kind, RIGHT, 3, 1)
                     ag_in(kind, LEFT, 3, 0)
 
         turn_w(i)
         for p in range(Q):
-            second(i, p)
-        return 0
-
-    obs_in(x_mate)
-    sight_on.start()
-    turn_by(2, 0)
-    obs_in((1 - h) * 2 + (1 - c))
-    turn_by(3, 0)
+            second(i, slice(p * ROWS, (p + 1) * ROWS))
+        return 0
+
     lax.fori_loop(0, Z, first_by, 0)
-    lax.fori_loop(0, Z - 1, second_by, 0)
+    lax.fori_loop(0, K - 1, second_by, 0)
     take_last(MID, K)
     head_core.start()
-    turn_w(Z - 1)
-    for p in range(Q):
-        second(Z - 1, p)
+    turn_w(K - 1)
 
     head_core_in()
     whp[...] = jnp.zeros_like(whp)
@@ -338,6 +342,8 @@
     for t in (2, 1, 3, 0):
         p = mate(t)
         rows = pl.ds(pl.multiple_of(p * ROWS, ROWS), ROWS)
+
+        second(K - 1, rows)
 
         def forward2(i, _):
             cols = pl.ds(pl.multiple_of(p * ROWS + i * 128, 128), 128)
@@ -516,7 +522,7 @@
             sib_s[b, j] = dI[b, j, 1 - c].astype(BF16)
     core_sum = copy(sib_s, sib_r, sb_s.at[8], sb_r.at[8], sib)
     core_sum.start()
-    lax.fori_loop(2, 4, middle, 0)
+    lax.fori_loop(2, 3, middle, 0)
     core_sum.wait_recv()
 
     def own_in(off, j):
@@ -571,9 +577,15 @@
         return 0
 
     lax.fori_loop(0, 2, join2, 0)
+    lax.fori_loop(3, 4, middle, 0)
     ri_put(RIGHT, 3, 0, True)
     ri_put(LEFT, 3, 1, True)
     lax.fori_loop(2, 4, join2, 0)
+    for j in range(2):
+        ri_put(RIGHT, 2, j, True)
+        ri_put(LEFT, 2, j, True)
+    lax.fori_loop(0, 2, ones, 0)
+    lax.fori_loop(2, 4, ones, 0)
     for off in (1, -1, 3, -3, K):
         dh_in(off)
     tot = dH[0].astype(F32)
@@ -588,11 +600,9 @@
     for t in (2, 1, 3):
         dh_mate(t).start()
 
-    lax.fori_loop(0, 2, ones, 0)
     for j in range(2):
-        ri_put(RIGHT, 2, j, True)
-        ri_put(LEFT, 2, j, True)
-    lax.fori_loop(2, 4, ones, 0)
+        ri_put(RIGHT, 1, j, True)
+        ri_put(LEFT, 1, j, True)
     for t in (2, 1, 3):
         p = mate(t)
         copy(dHg.at[p], dHg.at[p], gp_s.at[DH, p], gp_r.at[DH, p], sib).wait_recv()
@@ -603,14 +613,8 @@
     head_y.start()
     middle_end(0)
     middle_end(2)
-    for j in range(2):
-        ri_put(RIGHT, 1, j, True)
-        ri_put(LEFT, 1, j, True)
     middle_end(1)
     middle_end(3)
-    def chosen(got, own):
-        return jnp.where(jnp.full(own.shape, flag) == 1, got.astype(F32), own.astype(F32)).astype(BF16)
-
     for j in range(2):
         tin[j] = own_in(0, j) + ri_in(RIGHT, 0, j) + ri_in(LEFT, 0, j)
     xs[...] = tin[1 - h].astype(BF16)
@@ -621,6 +625,9 @@
     ni[...] = tin[h].astype(BF16)
     in_y = copy(ni, yi, y_s.at[4], y_r.at[4], after)
     in_y.start()
+    def chosen(got, own):
+        return jnp.where(jnp.full(own.shape, flag) == 1, got.astype(F32), own.astype(F32)).astype(BF16)
+
     head_y.wait_recv()
     o_head[...] = chosen(yh[...], nh[...])
     for t in (0, 1, 2, 3):
@@ -699,9 +706,9 @@
     out = pl.pallas_call(
         kernel,
         out_shape=(
-            jax.ShapeDtypeStruct((8, D), BF16),
-            jax.ShapeDtypeStruct((64, D), BF16),
-            jax.ShapeDtypeStruct((ACT, 64), BF16),
+            pltpu.VMEM((8, D), BF16),
+            pltpu.VMEM((64, D), BF16),
+            pltpu.VMEM((ACT, 64), BF16),
             jax.ShapeDtypeStruct((1,), F32),
             jax.ShapeDtypeStruct((1,), F32),
         ),
@@ -714,7 +721,7 @@
             V((Z, 2, 2, ACT, 64), BF16),
             V((Z, Q, 64, QC), BF16),
             V((D, OBS), BF16),
-            V((QC, BK), BF16),
+            V((2, QC, BK), BF16),
             V((D, OBS), F32),
             V((D, D), BF16),
             V((D, D), BF16),
@@ -763,7 +770,7 @@
             S((4,)),
         ],
         compiler_params=pltpu.CompilerParams(
-            collective_id=0, has_side_effects=True, vmem_limit_bytes=64 * 1024 * 1024 - 65536
+            collective_id=0, has_side_effects=True, vmem_limit_bytes=60 * 1024 * 1024
         ),
     )(observations[0], returns, actions, w_input[0], w_middle[0], w_head[0].T, log_rate, copy_from, perturb)
     return out[0][None], out[1][None], out[2].T[None], out[3], out[4]

time: 107 us -> 103 us (0.963)
  Pallas kernels: 99.4 us -> 97.1 us
  local copies, waits for them, and re-layouts: 3.65 us -> 1.91 us
    pallas_call x1, Pallas kernels: 99.4 us -> 97.1 us  [local(): pl.pallas_call(kernel, out_shape=(pltpu.VMEM((8, D), BF16), pltpu.VMEM((6...]
    unnamed x5 -> x3, local copies, waits for them, and re-layouts: 3.65 us -> 1.91 us
where the time goes in v3:
time: 103 us
  Pallas kernels  97.1 us (94%)
  between operations  4.09 us (4%)
  local copies, waits for them, and re-layouts  1.91 us (2%)
    pallas_call x1, Pallas kernels, local(): pl.pallas_call(kernel, out_shape=(pltpu.VMEM((8, D), BF16), pltpu.VMEM((6...  97.1 us

profile of v3, /device:TPU:1, one launch (start us, length us, event | category | flops | bytes accessed | tf_op | source)
XLA Modules:
  0.0 103.1 jit_solution(15983381774819025685)
XLA Ops:
  0.6 97.1 %shard_map.128 = (bf16[8,2048]{1,0:T(8,128)(2,1)S(1)}, bf16[64,2048]{1,0:T(8,128)(2,1)S(1)}, bf16[18,64]{1,0:T(8,128)(2,1)S(1)}, f32[1]{0:T(128)}, f32[1]{0:T(128)}) custom-call(bf16[512,256]{1,0:T(8,128)(2,1)} %bitcast.14, f32[1,512]{1,0:T(1,128)} %ret.1, s32[1,512]{1,0:T(1,128)} %act.1, bf16[8,2048]{1,0:T(8,128)(2,1)} %bitcast.16, ...), custom_call_target="tpu_custom_call" | custom-call | tf_op jit(solution)/shard_map/pallas_call | solution.py:706
  97.8 0.6 copy.19
  98.4 0.7 copy.20
  99.1 0.6 copy.21

commit v4 on v3

--- a/solution.py
+++ b/solution.py
@@ -315,6 +315,8 @@
                 for kind in MID:
                     ag_in(kind, RIGHT, 3, 1)
                     ag_in(kind, LEFT, 3, 0)
+                take_last(MID, K)
+                head_core.start()
 
         turn_w(i)
         for p in range(Q):
@@ -323,8 +325,6 @@
 
     lax.fori_loop(0, Z, first_by, 0)
     lax.fori_loop(0, K - 1, second_by, 0)
-    take_last(MID, K)
-    head_core.start()
     turn_w(K - 1)
 
     head_core_in()
@@ -502,7 +502,11 @@
 
     lax.fori_loop(2, 4, back, 0)
     lax.fori_loop(0, 2, join3, 0)
-    lax.fori_loop(4, 8, back, 0)
+    lax.fori_loop(2, 3, middle, 0)
+    lax.fori_loop(0, 2, join2, 0)
+    lax.fori_loop(4, 7, back, 0)
+    lax.fori_loop(2, 4, join2, 0)
+    lax.fori_loop(7, 8, back, 0)
 
     def turn_back(i, _):
         feats = pl.ds(pl.multiple_of(i * 256, 256), 256)
@@ -522,7 +526,7 @@
             sib_s[b, j] = dI[b, j, 1 - c].astype(BF16)
     core_sum = copy(sib_s, sib_r, sb_s.at[8], sb_r.at[8], sib)
     core_sum.start()
-    lax.fori_loop(2, 3, middle, 0)
+    lax.fori_loop(3, 4, middle, 0)
     core_sum.wait_recv()
 
     def own_in(off, j):
@@ -576,16 +580,13 @@
         rs_put(LEFT, 1, j, True)
         return 0
 
-    lax.fori_loop(0, 2, join2, 0)
-    lax.fori_loop(3, 4, middle, 0)
+    lax.fori_loop(0, 2, ones, 0)
     ri_put(RIGHT, 3, 0, True)
     ri_put(LEFT, 3, 1, True)
-    lax.fori_loop(2, 4, join2, 0)
+    lax.fori_loop(2, 4, ones, 0)
     for j in range(2):
         ri_put(RIGHT, 2, j, True)
         ri_put(LEFT, 2, j, True)
-    lax.fori_loop(0, 2, ones, 0)
-    lax.fori_loop(2, 4, ones, 0)
     for off in (1, -1, 3, -3, K):
         dh_in(off)
     tot = dH[0].astype(F32)
@@ -600,6 +601,10 @@
     for t in (2, 1, 3):
         dh_mate(t).start()
 
+    middle_end(0)
+    middle_end(2)
+    middle_end(1)
+    middle_end(3)
     for j in range(2):
         ri_put(RIGHT, 1, j, True)
         ri_put(LEFT, 1, j, True)
@@ -611,10 +616,6 @@
     nh[...] = (wh[z, h, c].astype(F32) - rate * jnp.transpose(tH[own_rows, :])[0:ACT, :]).astype(BF16)
     head_y = copy(nh, yh, y_s.at[5], y_r.at[5], after)
     head_y.start()
-    middle_end(0)
-    middle_end(2)
-    middle_end(1)
-    middle_end(3)
     for j in range(2):
         tin[j] = own_in(0, j) + ri_in(RIGHT, 0, j) + ri_in(LEFT, 0, j)
     xs[...] = tin[1 - h].astype(BF16)
@@ -628,8 +629,6 @@
     def chosen(got, own):
         return jnp.where(jnp.full(own.shape, flag) == 1, got.astype(F32), own.astype(F32)).astype(BF16)
 
-    head_y.wait_recv()
-    o_head[...] = chosen(yh[...], nh[...])
     for t in (0, 1, 2, 3):
         p = mate(t)
         own = nm.at[p] if t == 0 else om.at[p]
@@ -639,6 +638,8 @@
         o_mid[:, pl.ds(pl.multiple_of(p * QC, QC), QC)] = chosen(ym[p], own[...])
     pick = pert[m]
     o_rate[0] = jnp.where(flag == 1, lr_before, lr) + jnp.where(pick == 0, -0.2, jnp.where(pick == 1, 0.0, 0.2))
+    head_y.wait_recv()
+    o_head[...] = chosen(yh[...], nh[...])
     prior.wait_recv()
     cross.wait_recv()
     cross_y.wait_recv()

time: 103 us -> 101 us (0.981)
  Pallas kernels: 97.1 us -> 94.9 us
    pallas_call x1, Pallas kernels: 97.1 us -> 94.9 us  [local(): pl.pallas_call(kernel, out_shape=(pltpu.VMEM((8, D), BF16), pltpu.VMEM((6...]
where the time goes in v4:
time: 101 us
  Pallas kernels  94.9 us (94%)
  between operations  4.09 us (4%)
  local copies, waits for them, and re-layouts  1.91 us (2%)
    pallas_call x1, Pallas kernels, local(): pl.pallas_call(kernel, out_shape=(pltpu.VMEM((8, D), BF16), pltpu.VMEM((6...  94.9 us

profile of v4, /device:TPU:1, one launch (start us, length us, event | category | flops | bytes accessed | tf_op | source)
XLA Modules:
  0.0 100.9 jit_solution(6623483753320618319)
XLA Ops:
  0.6 94.9 %shard_map.128 = (bf16[8,2048]{1,0:T(8,128)(2,1)S(1)}, bf16[64,2048]{1,0:T(8,128)(2,1)S(1)}, bf16[18,64]{1,0:T(8,128)(2,1)S(1)}, f32[1]{0:T(128)}, f32[1]{0:T(128)}) custom-call(bf16[512,256]{1,0:T(8,128)(2,1)} %bitcast.14, f32[1,512]{1,0:T(1,128)} %ret.1, s32[1,512]{1,0:T(1,128)} %act.1, bf16[8,2048]{1,0:T(8,128)(2,1)} %bitcast.16, ...), custom_call_target="tpu_custom_call" | custom-call | tf_op jit(solution)/shard_map/pallas_call | solution.py:707
  95.5 0.6 copy.19
  96.1 0.7 copy.20
  96.9 0.6 copy.21

commit v5 on v4

--- a/solution.py
+++ b/solution.py
@@ -500,14 +500,12 @@
         rs_put(LEFT, 2, j, True)
         return 0
 
-    lax.fori_loop(2, 4, back, 0)
+    lax.fori_loop(2, 5, back, 0)
     lax.fori_loop(0, 2, join3, 0)
     lax.fori_loop(2, 3, middle, 0)
+    lax.fori_loop(5, 6, back, 0)
     lax.fori_loop(0, 2, join2, 0)
-    lax.fori_loop(4, 7, back, 0)
-    lax.fori_loop(2, 4, join2, 0)
-    lax.fori_loop(7, 8, back, 0)
-
+    lax.fori_loop(6, 8, back, 0)
     def turn_back(i, _):
         feats = pl.ds(pl.multiple_of(i * 256, 256), 256)
         x = 0.5 * jnp.transpose(dT[feats, :])
@@ -526,6 +524,7 @@
             sib_s[b, j] = dI[b, j, 1 - c].astype(BF16)
     core_sum = copy(sib_s, sib_r, sb_s.at[8], sb_r.at[8], sib)
     core_sum.start()
+    lax.fori_loop(2, 4, join2, 0)
     lax.fori_loop(3, 4, middle, 0)
     core_sum.wait_recv()
 

time: 101 us -> 99.8 us (0.988)
  Pallas kernels: 94.9 us -> 93.7 us
    pallas_call x1, Pallas kernels: 94.9 us -> 93.7 us  [local(): pl.pallas_call(kernel, out_shape=(pltpu.VMEM((8, D), BF16), pltpu.VMEM((6...]
where the time goes in v5:
time: 99.8 us; the launch traced here: 99.7 us
  Pallas kernels  93.7 us (94%)
  between operations  4.09 us (4%)
  local copies, waits for them, and re-layouts  1.91 us (2%)
    pallas_call x1, Pallas kernels, local(): pl.pallas_call(kernel, out_shape=(pltpu.VMEM((8, D), BF16), pltpu.VMEM((6...  93.7 us

profile of v5, /device:TPU:1, one launch (start us, length us, event | category | flops | bytes accessed | tf_op | source)
XLA Modules:
  0.0 99.7 jit_solution(12571443326310432713)
XLA Ops:
  0.6 93.7 %shard_map.128 = (bf16[8,2048]{1,0:T(8,128)(2,1)S(1)}, bf16[64,2048]{1,0:T(8,128)(2,1)S(1)}, bf16[18,64]{1,0:T(8,128)(2,1)S(1)}, f32[1]{0:T(128)}, f32[1]{0:T(128)}) custom-call(bf16[512,256]{1,0:T(8,128)(2,1)} %bitcast.14, f32[1,512]{1,0:T(1,128)} %ret.1, s32[1,512]{1,0:T(1,128)} %act.1, bf16[8,2048]{1,0:T(8,128)(2,1)} %bitcast.16, ...), custom_call_target="tpu_custom_call" | custom-call | tf_op jit(solution)/shard_map/pallas_call | solution.py:706
  94.3 0.6 copy.19
  94.9 0.7 copy.20
  95.6 0.6 copy.21
